TPU v7x, 32 devices: a whole 2x2x4 slice. The times are simulated.
32 devices in a mesh: row: 8 (over z, x), col: 4 (over y, core).
Axes of the slice: x: 2, y: 2, z: 4, core: 2. Of those that a mesh axis runs over, the one named last changes fastest.
Arguments:
- offsets: int32 [8, 4, 2], P('row', 'col'), may hold values from 1 to 3
- targets: float32 [3, 3, 256, 512], P(None, None, 'row', 'col'), may hold values from -60 to 60
- grid_fine: float32 [32, 256, 512], P(None, 'row', 'col'), may hold values from -6 to 6
- grid_coarse: float32 [32, 64, 128], P(None, 'row', 'col'), may hold values from -6 to 6
- weight_in: float32 [512, 64], replicated, may hold values from -0.75 to 0.75
- weight_mid: float32 [1, 512, 512], replicated, may hold values from -0.25 to 0.25
- weight_out: float32 [3, 512], replicated, may hold values from -0.397747564 to 0.397747564
- fine_first: float32 [32, 256, 512], P(None, 'row', 'col'), may hold values from -0.012 to 0.012
- fine_second: float32 [32, 256, 512], P(None, 'row', 'col'), may hold values from 1e-06 to 0.0001
- coarse_first: float32 [32, 64, 128], P(None, 'row', 'col'), may hold values from -0.012 to 0.012
- coarse_second: float32 [32, 64, 128], P(None, 'row', 'col'), may hold values from 1e-06 to 0.0001
- in_first: float32 [512, 64], replicated, may hold values from -0.012 to 0.012
- in_second: float32 [512, 64], replicated, may hold values from 1e-06 to 0.0001
- mid_first: float32 [1, 512, 512], replicated, may hold values from -0.012 to 0.012
- mid_second: float32 [1, 512, 512], replicated, may hold values from 1e-06 to 0.0001
- out_first: float32 [3, 512], replicated, may hold values from -0.012 to 0.012
- out_second: float32 [3, 512], replicated, may hold values from 1e-06 to 0.0001
Outputs:
- fine_step: float32 [32, 256, 512], P(None, 'row', 'col')
- coarse_step: float32 [32, 64, 128], P(None, 'row', 'col')
- input_step: float32 [512, 64], replicated
- middle_step: float32 [1, 512, 512], replicated
- output_step: float32 [3, 512], replicated
All inputs are finite; a program needn't handle non-finite values.
Results may differ from a plain program's by a relative error of at most 0.0014.
The roundings to bfloat16 on the way count: a program that leaves them out, or rounds other values in their place, can miss the bound.
Values sent between devices are 32-bit elements; how exact they have to be, the bound alone decides.
A program may use at most 64 MiB of HBM per device.

v0:
```python
import functools

import jax
import jax.numpy as jnp
from jax import lax
from jax.experimental import pallas as pl
from jax.experimental.pallas import tpu as pltpu
from jax.sharding import PartitionSpec as P

SUB = 4
RATIO = 4
ADAM_STEP = 10


BETA_ONE = 0.9
BETA_TWO = 0.99
ADAM_EPSILON = 1e-08
CLIP_RMS = 0.01
LOSS_VALUE = 0.25
MEAN_EPSILON = 1e-06


def shifted(block, axis, distance):
    devices = range(lax.axis_size(axis))
    route = [(i - distance, i) for i in devices if i - distance in devices]
    return lax.ppermute(block, axis, route)


def interp_table(samples, level_ratio, offset):
    positions = jnp.arange(samples, dtype=jnp.int32)
    base_index = positions // level_ratio
    fraction = (
        (positions % level_ratio).astype(jnp.float32) + offset.astype(jnp.float32) / SUB
    ) / level_ratio
    column = jnp.arange(samples // level_ratio + 1, dtype=jnp.int32)
    lower_hit = (column[None, :] == base_index[:, None]).astype(jnp.float32)
    upper_hit = (column[None, :] == base_index[:, None] + 1).astype(jnp.float32)
    return lower_hit * (1.0 - fraction)[:, None] + upper_hit * fraction[:, None]


def level_tables(row_count, col_count, shift_y, shift_x):
    return (
        interp_table(row_count, 1, shift_y),
        interp_table(col_count, 1, shift_x),
        interp_table(row_count, RATIO, shift_y),
        interp_table(col_count, RATIO, shift_x),
    )


def sample_level(extended, row_table, col_table):
    across = jnp.einsum("kjl,ml->kjm", extended, col_table, precision=lax.Precision.HIGHEST)
    return jnp.einsum("ij,kjm->kim", row_table, across, precision=lax.Precision.HIGHEST)


def spread_level(cotangent, row_table, col_table):
    backward = jnp.einsum("ij,kim->kjm", row_table, cotangent, precision=lax.Precision.HIGHEST)
    return jnp.einsum("kjm,ml->kjl", backward, col_table, precision=lax.Precision.HIGHEST)


def sample_features(fine_ext, coarse_ext, tables):
    fine_feat = sample_level(fine_ext, tables[0], tables[1])
    coarse_feat = sample_level(coarse_ext, tables[2], tables[3])
    channels, row_count, col_count = fine_feat.shape
    return jnp.concatenate(
        [
            fine_feat.reshape(channels, row_count * col_count),
            coarse_feat.reshape(channels, row_count * col_count),
        ],
        axis=0,
    ).astype(jnp.bfloat16)


def spread_features(feature_grad, tables):
    channels = feature_grad.shape[0] // 2
    row_count = tables[0].shape[0]
    col_count = tables[1].shape[0]
    fine_cot = feature_grad[:channels].reshape(channels, row_count, col_count)
    coarse_cot = feature_grad[channels:].reshape(channels, row_count, col_count)
    return (
        spread_level(fine_cot, tables[0], tables[1]),
        spread_level(coarse_cot, tables[2], tables[3]),
    )


def matmul(former, latter):
    return jnp.dot(former, latter, preferred_element_type=jnp.float32)


def contract_rows(former, latter):
    return lax.dot_general(
        former, latter, (((0,), (0,)), ((), ())), preferred_element_type=jnp.float32
    )


def contract_cols(former, latter):
    return lax.dot_general(
        former, latter, (((1,), (1,)), ((), ())), preferred_element_type=jnp.float32
    )


def silu_slope(pre_act):
    sigmoid = jax.nn.sigmoid(pre_act)
    return sigmoid * (1.0 + pre_act * (1.0 - sigmoid))


def decoder_forward(features, low_in, low_mid, low_out):
    pre_acts = [matmul(low_in, features)]
    activations = [jax.nn.silu(pre_acts[0]).astype(jnp.bfloat16)]
    pre_acts.append(matmul(low_mid[0], activations[-1]))
    activations.append(jax.nn.silu(pre_acts[-1]).astype(jnp.bfloat16))
    return (matmul(low_out, activations[-1]), pre_acts, activations)


def decoder_backward(features, pre_acts, activations, cotangent, low_in, low_mid, low_out):
    out_cotangent = cotangent.astype(jnp.bfloat16)
    grad_out = contract_cols(out_cotangent, activations[-1])
    upward = contract_rows(low_out, out_cotangent)
    grads_mid = []
    delta_low = (upward * silu_slope(pre_acts[1])).astype(jnp.bfloat16)
    grads_mid.insert(0, contract_cols(delta_low, activations[0]))
    upward = contract_rows(low_mid[0], delta_low)
    delta_low = (upward * silu_slope(pre_acts[0])).astype(jnp.bfloat16)
    grad_in = contract_cols(delta_low, features)
    feature_grad = contract_rows(low_in, delta_low)
    return (grad_in, jnp.stack(grads_mid), grad_out, feature_grad)


def pixel_cotangent(value_error, row_error, row_prior, col_error, col_prior):
    return (
        2.0 * LOSS_VALUE * value_error
        + 2.0 * (row_prior - row_error)
        + 2.0 * (col_prior - col_error)
    )


def clip_factor(total, entries):
    return jnp.minimum(1.0, CLIP_RMS / jnp.sqrt(total / entries + MEAN_EPSILON))


def adam_step(gradient, moment_one, moment_two, clip_scale):
    clipped = gradient * clip_scale
    new_one = BETA_ONE * moment_one + (1.0 - BETA_ONE) * clipped
    new_two = BETA_TWO * moment_two + (1.0 - BETA_TWO) * clipped * clipped
    return (
        new_one
        / (1.0 - BETA_ONE**ADAM_STEP)
        / (jnp.sqrt(new_two / (1.0 - BETA_TWO**ADAM_STEP)) + ADAM_EPSILON)
    )


MESH = pl.DeviceIdType.MESH
LANES = 128
SUBLANES = 8


def decoder_kernel(
    used,
    mid_ref,
    rest_ref,
    mid_first_hbm,
    mid_second_hbm,
    rest_first_ref,
    rest_second_ref,
    mid_step_ref,
    rest_step_ref,
    total_ref,
    mine_ref,
    sum_ref,
    from_pair,
    paired,
    arrived,
    own,
    pair_send,
    pair_recv,
    send,
    recv,
    mid_first_ref,
    mid_second_ref,
    load_sem,
):
    row, col = lax.axis_index("row"), lax.axis_index("col")
    chips = mine_ref.shape[1]
    half_cols = lax.axis_size("col") // 2
    core = lax.rem(col, 2)
    chip = row * half_cols + lax.div(col, 2)
    pair = (row, col + 1 - 2 * core)

    def place(step):
        other = lax.rem(chip + step, chips)
        return other, (lax.div(other, half_cols), lax.rem(other, half_cols) * 2 + core)

    def pair_copy(slot, source, target):
        return pltpu.make_async_remote_copy(
            src_ref=source,
            dst_ref=target,
            send_sem=pair_send.at[slot],
            recv_sem=pair_recv.at[slot],
            device_id=pair,
            device_id_type=MESH,
        )

    def block_copy(step):
        other, device = place(step)
        return pltpu.make_async_remote_copy(
            src_ref=paired.at[other],
            dst_ref=arrived.at[step],
            send_sem=send.at[0, step],
            recv_sem=recv.at[0, step],
            device_id=device,
            device_id_type=MESH,
        )

    def result_copy(step):
        _, device = place(step)
        return pltpu.make_async_remote_copy(
            src_ref=own,
            dst_ref=sum_ref.at[core, chip],
            send_sem=send.at[1, step],
            recv_sem=recv.at[1, step],
            device_id=device,
            device_id_type=MESH,
        )

    barrier = pltpu.get_barrier_semaphore()
    pl.semaphore_signal(barrier, inc=1, device_id=pair, device_id_type=MESH)

    @pl.loop(1, chips)
    def _(step):
        _, device = place(step)
        pl.semaphore_signal(barrier, inc=1, device_id=device, device_id_type=MESH)

    loads = (
        pltpu.make_async_copy(mid_first_hbm, mid_first_ref, load_sem.at[0]),
        pltpu.make_async_copy(mid_second_hbm, mid_second_ref, load_sem.at[1]),
    )
    for load in loads:
        load.start()
    hidden, mids = mid_ref.shape
    rows, lanes = mine_ref.shape[2:]
    rests = lanes - mids
    blocks = hidden // rows
    for block in range(2 * chips):
        where = divmod(block, chips)
        if block < blocks:
            span = slice(block * rows, (block + 1) * rows)
            mine_ref[where[0], where[1], :, :mids] = mid_ref[span, :]
            mine_ref[where[0], where[1], :, mids:] = rest_ref[span, :]
        else:
            mine_ref[where[0], where[1]] = jnp.zeros((rows, lanes), jnp.float32)

    pl.semaphore_wait(barrier, chips)

    first = pair_copy(0, mine_ref.at[1 - core], from_pair)
    first.start()
    first.wait()

    @pl.loop(1, chips)
    def _(step):
        other, _ = place(step)
        paired[other] = mine_ref[core, other] + from_pair[other]
        block_copy(step).start()

    own[...] = mine_ref[core, chip] + from_pair[chip]

    @pl.loop(1, chips)
    def _(step):
        block_copy(step).wait()
        own[...] += arrived[step]

    @pl.loop(1, chips)
    def _(step):
        result_copy(step).start()

    sum_ref[core, chip] = own[...]

    @pl.loop(1, chips)
    def _(step):
        result_copy(step).wait()

    last = pair_copy(1, sum_ref.at[core], sum_ref.at[core])
    last.start()
    last.wait()

    for load in loads:
        load.wait()
    total_ref[...] = sum_ref[0, 0, :SUBLANES, mids:]
    kept = lax.broadcasted_iota(jnp.int32, (rows, rests), 1) < used
    mid_squares = jnp.zeros((rows, mids), jnp.float32)
    rest_squares = jnp.zeros((rows, rests), jnp.float32)
    for block in range(blocks):
        where = divmod(block, chips)
        mid = sum_ref[where[0], where[1], :, :mids]
        rest = sum_ref[where[0], where[1], :, mids:]
        mid_squares += mid * mid
        rest_squares += jnp.where(kept, rest * rest, 0.0)
    total = jnp.sum(mid_squares, keepdims=True) + jnp.sum(rest_squares, keepdims=True)
    scale = clip_factor(total, hidden * (mids + used))
    for block in range(blocks):
        where = divmod(block, chips)
        span = slice(block * rows, (block + 1) * rows)
        mid_step_ref[span, :] = adam_step(
            sum_ref[where[0], where[1], :, :mids],
            mid_first_ref[span, :],
            mid_second_ref[span, :],
            scale,
        )
        rest_step_ref[span, :] = adam_step(
            sum_ref[where[0], where[1], :, mids:],
            rest_first_ref[span, :],
            rest_second_ref[span, :],
            scale,
        )


def decoder_steps(gradients, firsts, seconds, grid_local):
    grad_in, grad_mid, grad_out = gradients
    devices = lax.axis_size("row") * lax.axis_size("col")
    chips = devices // 2
    hidden, inputs = grad_in.shape
    outputs = grad_out.shape[0]
    mids = grad_mid.shape[2]
    used = inputs + outputs
    rests = -(-(used + 1) // LANES) * LANES
    rows = -(-hidden // (devices * SUBLANES)) * SUBLANES

    def beside(block_in, block_out, fill):
        column = jnp.full((hidden, rests - used), fill, jnp.float32)
        return jnp.concatenate([block_in, block_out.T, column], axis=1)

    shape = (2, chips, rows, mids + rests)
    flat = jax.ShapeDtypeStruct((hidden, mids), jnp.float32)
    side = jax.ShapeDtypeStruct((hidden, rests), jnp.float32)
    mid_step, rest_step, total = pl.pallas_call(
        functools.partial(decoder_kernel, used),
        out_shape=(flat, side, jax.ShapeDtypeStruct((SUBLANES, rests), jnp.float32)),
        in_specs=[
            pl.BlockSpec(memory_space=pl.ANY if place in (2, 3) else pltpu.VMEM) for place in range(6)
        ],
        out_specs=(pl.BlockSpec(memory_space=pltpu.VMEM),) * 3,
        scratch_shapes=[
            pltpu.VMEM(shape, jnp.float32),
            pltpu.VMEM(shape, jnp.float32),
            pltpu.VMEM(shape[1:], jnp.float32),
            pltpu.VMEM(shape[1:], jnp.float32),
            pltpu.VMEM(shape[1:], jnp.float32),
            pltpu.VMEM(shape[2:], jnp.float32),
            pltpu.SemaphoreType.DMA((2,)),
            pltpu.SemaphoreType.DMA((2,)),
            pltpu.SemaphoreType.DMA((2, chips)),
            pltpu.SemaphoreType.DMA((2, chips)),
            pltpu.VMEM((hidden, mids), jnp.float32),
            pltpu.VMEM((hidden, mids), jnp.float32),
            pltpu.SemaphoreType.DMA((2,)),
        ],
        compiler_params=pltpu.CompilerParams(collective_id=0, has_side_effects=True),
    )(
        grad_mid[0],
        beside(grad_in, grad_out, grid_local),
        firsts[1][0],
        seconds[1][0],
        beside(firsts[0], firsts[2], 0.0),
        beside(seconds[0], seconds[2], 1.0),
    )
    return (
        rest_step[:, :inputs],
        mid_step[None],
        rest_step[:, inputs:used].T,
        total[0, used],
    )


def shards(
    offsets,
    targets,
    grid_fine,
    grid_coarse,
    weight_in,
    weight_mid,
    weight_out,
    fine_first,
    fine_second,
    coarse_first,
    coarse_second,
    in_first,
    in_second,
    mid_first,
    mid_second,
    out_first,
    out_second,
):
    channels, sample_rows, sample_cols = grid_fine.shape
    coarse_rows = grid_coarse.shape[1]
    coarse_cols = grid_coarse.shape[2]
    low_in = weight_in.astype(jnp.bfloat16)
    low_mid = weight_mid.astype(jnp.bfloat16)
    low_out = weight_out.astype(jnp.bfloat16)
    top_rows = jnp.concatenate([grid_fine[:, :1, :], grid_coarse[:, :1, :]], axis=2)
    top_rows = shifted(top_rows, "row", -1)
    fine_tall = jnp.concatenate([grid_fine, top_rows[:, :, :sample_cols]], axis=1)
    coarse_tall = jnp.concatenate([grid_coarse, top_rows[:, :, sample_cols:]], axis=1)
    edge_cols = jnp.concatenate([fine_tall[:, :, :1], coarse_tall[:, :, :1]], axis=1)
    edge_cols = shifted(edge_cols, "col", -1)
    fine_ext = jnp.concatenate([fine_tall, edge_cols[:, : sample_rows + 1, :]], axis=2)
    coarse_ext = jnp.concatenate([coarse_tall, edge_cols[:, sample_rows + 1 :, :]], axis=2)
    tables = level_tables(sample_rows, sample_cols, offsets[0, 0, 0], offsets[0, 0, 1])
    features = sample_features(fine_ext, coarse_ext, tables)
    predicted, pre_acts, activations = decoder_forward(features, low_in, low_mid, low_out)
    outputs = predicted.shape[0]
    predicted = predicted.reshape(outputs, sample_rows, sample_cols)
    below = shifted(predicted[:, :1, :], "row", -1)
    beside = shifted(predicted[:, :, :1], "col", -1)
    above = jnp.concatenate([predicted[:, -1:, :], targets[1][:, -1:, :]], axis=0)
    above = shifted(above, "row", 1)
    before = jnp.concatenate([predicted[:, :, -1:], targets[2][:, :, -1:]], axis=0)
    before = shifted(before, "col", 1)
    row_global = lax.axis_index("row") * sample_rows + jnp.arange(sample_rows, dtype=jnp.int32)
    col_global = lax.axis_index("col") * sample_cols + jnp.arange(sample_cols, dtype=jnp.int32)
    row_valid = (row_global < lax.axis_size("row") * sample_rows - 1)[None, :, None]
    col_valid = (col_global < lax.axis_size("col") * sample_cols - 1)[None, None, :]
    row_next = jnp.concatenate([predicted[:, 1:, :], below], axis=1)
    col_next = jnp.concatenate([predicted[:, :, 1:], beside], axis=2)
    value_error = predicted - targets[0]
    row_error = jnp.where(row_valid, row_next - predicted - targets[1], 0.0)
    col_error = jnp.where(col_valid, col_next - predicted - targets[2], 0.0)
    above = jnp.where(
        lax.axis_index("row") > 0, predicted[:, :1, :] - above[:outputs] - above[outputs:], 0.0
    )
    before = jnp.where(
        lax.axis_index("col") > 0, predicted[:, :, :1] - before[:outputs] - before[outputs:], 0.0
    )
    row_prior = jnp.concatenate([above, row_error[:, :-1, :]], axis=1)
    col_prior = jnp.concatenate([before, col_error[:, :, :-1]], axis=2)
    cotangent = pixel_cotangent(value_error, row_error, row_prior, col_error, col_prior)
    grad_in, grad_mid, grad_out, feature_grad = decoder_backward(
        features,
        pre_acts,
        activations,
        cotangent.reshape(outputs, sample_rows * sample_cols),
        low_in,
        low_mid,
        low_out,
    )
    fine_back, coarse_back = spread_features(feature_grad, tables)
    side_cols = jnp.concatenate(
        [fine_back[:, :, sample_cols:], coarse_back[:, :, coarse_cols:]], axis=1
    )
    side_cols = shifted(side_cols, "col", 1)
    fine_tall_grad = jnp.concatenate(
        [fine_back[:, :, :1] + side_cols[:, : sample_rows + 1, :], fine_back[:, :, 1:sample_cols]],
        axis=2,
    )
    coarse_tall_grad = jnp.concatenate(
        [
            coarse_back[:, :, :1] + side_cols[:, sample_rows + 1 :, :],
            coarse_back[:, :, 1:coarse_cols],
        ],
        axis=2,
    )
    bottom_rows = jnp.concatenate(
        [fine_tall_grad[:, sample_rows:, :], coarse_tall_grad[:, coarse_rows:, :]], axis=2
    )
    bottom_rows = shifted(bottom_rows, "row", 1)
    fine_grad = jnp.concatenate(
        [
            fine_tall_grad[:, :1, :] + bottom_rows[:, :, :sample_cols],
            fine_tall_grad[:, 1:sample_rows, :],
        ],
        axis=1,
    )
    coarse_grad = jnp.concatenate(
        [
            coarse_tall_grad[:, :1, :] + bottom_rows[:, :, sample_cols:],
            coarse_tall_grad[:, 1:coarse_rows, :],
        ],
        axis=1,
    )
    grid_local = jnp.sum(fine_grad * fine_grad) + jnp.sum(coarse_grad * coarse_grad)
    devices = lax.axis_size("row") * lax.axis_size("col")
    grid_entries = (fine_grad.size + coarse_grad.size) * devices
    input_step, middle_step, output_step, grid_total = decoder_steps(
        (grad_in, grad_mid, grad_out),
        (in_first, mid_first, out_first),
        (in_second, mid_second, out_second),
        grid_local,
    )
    grid_scale = clip_factor(grid_total, grid_entries)
    fine_step = adam_step(fine_grad, fine_first, fine_second, grid_scale)
    coarse_step = adam_step(coarse_grad, coarse_first, coarse_second, grid_scale)
    return (fine_step, coarse_step, input_step, middle_step, output_step)


def solution(mesh):
    placed = (
        P("row", "col", None),
        P(None, None, "row", "col"),
        P(None, "row", "col"),
        P(None, "row", "col"),
        P(),
        P(),
        P(),
        P(None, "row", "col"),
        P(None, "row", "col"),
        P(None, "row", "col"),
        P(None, "row", "col"),
        P(),
        P(),
        P(),
        P(),
        P(),
        P(),
    )
    return jax.shard_map(
        shards,
        mesh=mesh,
        in_specs=placed,
        out_specs=(P(None, "row", "col"), P(None, "row", "col"), P(), P(), P()),
        check_vma=False,
    )
```

profile of v0, /device:TPU:27, one launch (start us, length us, event | category | flops | bytes accessed | tf_op | source)
XLA Modules:
  0.0 146.0 jit_solution(13654999486104871175)
XLA Ops:
  0.6 1.0 copy.102
  1.6 0.9 slice.148
  2.6 2.2 %collective-permute-start = (f32[32,1,160]{2,1,0:T(1,128)S(1)}, f32[32,1,160]{2,1,0:T(1,128)S(1)}, u32[]{:S(2)}, u32[]{:S(2)}) collective-permute-start(f32[32,1,160]{2,1,0:T(1,128)S(1)} %copy.103), channel_id=1, source_target_pairs={{4,0},{8,4},{12,8},{16,12},{20,16},{24,20},{28,24},{5,1},{9,5},{13... | collective-permute-start | bytes 61448 | tf_op jit(solution)/shard_map/ppermute | solution.py:26
  4.8 1.3 fusion.134
  7.5 0.9 slice_bitcast_fusion.3
  8.4 0.8 copy.122
  9.2 0.8 copy.124
  10.1 1.0 copy.123
  11.1 1.0 copy.125
  12.3 1.0 maximum_maximum_fusion.1
  14.2 2.9 %collective-permute-start.1 = (f32[32,42,1]{1,0,2:T(8,128)S(1)}, f32[32,42,1]{1,0,2:T(8,128)S(1)}, u32[]{:S(2)}, u32[]{:S(2)}) collective-permute-start(f32[32,42,1]{1,0,2:T(8,128)S(1)} %pad_maximum_fusion.7), channel_id=1, source_target_pairs={{1,0},{2,1},{3,2},{5,4},{6,5},{7,6},{9,8},{10,9},{11,10},{13,12},{... | collective-permute-start | bytes 16136 | tf_op jit(solution)/shard_map/ppermute | solution.py:26
  17.1 2.4 %collective-permute-done.1 = f32[32,42,1]{1,0,2:T(8,128)S(1)} collective-permute-done((f32[32,42,1]{1,0,2:T(8,128)S(1)}, f32[32,42,1]{1,0,2:T(8,128)S(1)}, u32[]{:S(2)}, u32[]{:S(2)}) %collective-permute-start.1) | collective-permute-done | bytes 5408 | tf_op jit(solution)/shard_map/ppermute | solution.py:26
  20.3 1.2 fusion.14
  21.5 0.6 convolution_convert_fusion.1
  22.6 0.6 convolution_convert_fusion
  23.3 4.6 %fusion.11 = (bf16[512,4096]{0,1:T(8,128)(2,1)S(1)}, f32[4096,512]{1,0:T(8,128)}) fusion(bf16[64,4096]{1,0:T(8,128)(2,1)S(1)} %bitcast_dynamic-update-slice_fusion, f32[512,64]{0,1:T(8,128)S(1)} %copy-done.7), kind=kOutput, calls=%fused_computation.19 | convolution fusion | flops 278953984 | bytes 13238272 | tf_op jit(solution)/shard_map/dot_general | solution.py:86
  27.9 4.6 %fusion.5 = (bf16[512,4096]{0,1:T(8,128)(2,1)S(1)}, f32[4096,512]{1,0:T(8,128)}) fusion(bf16[512,4096]{0,1:T(8,128)(2,1)S(1)} %get-tuple-element.50, f32[1,512,512]{2,1,0:T(8,128)S(1)} %copy-done.13), kind=kOutput, calls=%fused_computation.10 | convolution fusion | flops 2158231552 | bytes 17825792 | tf_op jit(solution)/shard_map/dot_general | solution.py:86
  32.6 2.0 %copy-done.2 = bf16[512,4096]{0,1:T(8,128)(2,1)} copy-done((bf16[512,4096]{0,1:T(8,128)(2,1)}, bf16[512,4096]{0,1:T(8,128)(2,1)S(1)}, u32[]{:S(2)}) %copy-start.2) | copy-done | bytes 4194328
  34.5 1.2 fusion.113
  35.8 1.9 %collective-permute-start.4 = (f32[6,32,1]{2,1,0:T(8,128)S(1)}, f32[6,32,1]{2,1,0:T(8,128)S(1)}, u32[]{:S(2)}, u32[]{:S(2)}) collective-permute-start(f32[6,32,1]{2,1,0:T(8,128)S(1)} %pad_maximum_fusion.2), channel_id=1, source_target_pairs={{0,1},{1,2},{2,3},{4,5},{5,6},{6,7},{8,9},{9,10},{10,11},{12,13},{... | collective-permute-start | bytes 2312 | tf_op jit(solution)/shard_map/ppermute | solution.py:26
  37.9 1.5 %collective-permute-done.4 = f32[6,32,1]{2,1,0:T(8,128)S(1)} collective-permute-done((f32[6,32,1]{2,1,0:T(8,128)S(1)}, f32[6,32,1]{2,1,0:T(8,128)S(1)}, u32[]{:S(2)}, u32[]{:S(2)}) %collective-permute-start.4) | collective-permute-done | bytes 800 | tf_op jit(solution)/shard_map/ppermute | solution.py:26
  39.4 1.9 %collective-permute-start.5 = (f32[3,32,1]{2,1,0:T(8,128)S(1)}, f32[3,32,1]{2,1,0:T(8,128)S(1)}, u32[]{:S(2)}, u32[]{:S(2)}) collective-permute-start(f32[3,32,1]{2,1,0:T(8,128)S(1)} %get-tuple-element.47), channel_id=1, source_target_pairs={{1,0},{2,1},{3,2},{5,4},{6,5},{7,6},{9,8},{10,9},{11,10},{13,12},{... | collective-permute-start | bytes 1160 | tf_op jit(solution)/shard_map/ppermute | solution.py:26
  41.4 1.3 collective-permute-start.2
  42.7 3.0 %collective-permute-done.5 = f32[3,32,1]{2,1,0:T(8,128)S(1)} collective-permute-done((f32[3,32,1]{2,1,0:T(8,128)S(1)}, f32[3,32,1]{2,1,0:T(8,128)S(1)}, u32[]{:S(2)}, u32[]{:S(2)}) %collective-permute-start.5) | collective-permute-done | bytes 416 | tf_op jit(solution)/shard_map/ppermute | solution.py:26
  45.9 4.1 %collective-permute-start.3 = (f32[3,1,128]{2,1,0:T(1,128)S(1)}, f32[3,1,128]{2,1,0:T(1,128)S(1)}, u32[]{:S(2)}, u32[]{:S(2)}) collective-permute-start(f32[3,1,128]{2,1,0:T(1,128)S(1)} %get-tuple-element.45), channel_id=1, source_target_pairs={{4,0},{8,4},{12,8},{16,12},{20,16},{24,20},{28,24},{5,1},{9,5},{13... | collective-permute-start | bytes 4616 | tf_op jit(solution)/shard_map/ppermute | solution.py:26
  50.1 0.5 collective-permute-done.3
  50.9 5.8 %fusion.1 = bf16[512,4096]{0,1:T(8,128)(2,1)S(1)} fusion(f32[4096,512]{1,0:T(8,128)} %get-tuple-element.53, bf16[3,4096]{1,0:T(4,128)(2,1)S(1)} %fusion.53, f32[3,512]{1,0:T(4,128)S(1)} %copy-done.12), kind=kOutput, calls=%fused_computation.3 | convolution fusion | flops 31458816 | bytes 12613632 | tf_op jit(solution)/shard_map/dot_general | solution.py:90
  56.7 3.3 %fusion.135.mid_ref = f32[512,512]{1,0:T(8,128)} fusion(bf16[512,4096]{0,1:T(8,128)(2,1)S(1)} %fusion.1, bf16[512,4096]{0,1:T(8,128)(2,1)S(1)} %copy-done.1), kind=kOutput, calls=%fused_computation.229 | convolution fusion | flops 2147483648 | bytes 9437184 | tf_op jit(solution)/shard_map/dot_general | solution.py:96
  60.0 3.6 %fusion = bf16[512,4096]{0,1:T(8,128)(2,1)S(1)} fusion(f32[4096,512]{1,0:T(8,128)S(1)} %bitcast.230, bf16[512,4096]{0,1:T(8,128)(2,1)S(1)} %fusion.1, f32[1,512,512]{2,1,0:T(8,128)S(1)} %copy-done.13), kind=kOutput, calls=%fused_computation.1 | convolution fusion | flops 2166620160 | bytes 17825792 | tf_op jit(solution)/shard_map/dot_general | solution.py:90
  63.6 1.4 convolution_bitcast_fusion
  65.1 0.5 copy-done.3
  65.7 0.8 convolution_bitcast_fusion.1
  66.5 1.2 fusion.46
  69.4 6.2 %collective-permute-start.6 = (f32[32,42,1]{1,0,2:T(8,128)S(1)}, f32[32,42,1]{1,0,2:T(8,128)S(1)}, u32[]{:S(2)}, u32[]{:S(2)}) collective-permute-start(f32[32,42,1]{1,0,2:T(8,128)S(1)} %pad_maximum_fusion.8), channel_id=1, source_target_pairs={{0,1},{1,2},{2,3},{4,5},{5,6},{6,7},{8,9},{9,10},{10,11},{12,13},{... | collective-permute-start | bytes 16136 | tf_op jit(solution)/shard_map/ppermute | solution.py:26
  75.6 3.6 %fusion.136 = f32[512,64]{1,0:T(8,128)S(1)} fusion(bf16[512,4096]{0,1:T(8,128)(2,1)} %copy-done.3, bf16[64,4096]{1,0:T(8,128)(2,1)} %copy-done.10), kind=kOutput, calls=%fused_computation.230 | convolution fusion | flops 268435456 | bytes 4849664 | tf_op jit(solution)/shard_map/dot_general | solution.py:96
  81.2 1.5 %collective-permute-start.7 = (f32[32,1,160]{2,1,0:T(1,128)S(1)}, f32[32,1,160]{2,1,0:T(1,128)S(1)}, u32[]{:S(2)}, u32[]{:S(2)}) collective-permute-start(f32[32,1,160]{2,1,0:T(1,128)S(1)} %fusion.74), channel_id=1, source_target_pairs={{0,4},{4,8},{8,12},{12,16},{16,20},{20,24},{24,28},{1,5},{5,9},{9,... | collective-permute-start | bytes 61448 | tf_op jit(solution)/shard_map/ppermute | solution.py:26
  82.7 3.5 %fusion.137 = f32[512,3]{1,0:T(8,128)S(1)} fusion(bf16[512,4096]{0,1:T(8,128)(2,1)} %copy-done.2, bf16[3,4096]{1,0:T(4,128)(2,1)} %copy-done.11), kind=kOutput, calls=%fused_computation.231 | convolution fusion | flops 12582912 | bytes 4225024 | tf_op jit(solution)/shard_map/dot_general | solution.py:96
  86.5 0.7 multiply_reduce_fusion.1
  87.3 0.8 multiply_reduce_fusion
  89.5 0.8 maximum_maximum_fusion.rest_ref
  90.3 46.0 %shard_map.200 = (f32[512,512]{1,0:T(8,128)}, f32[512,128]{1,0:T(8,128)}, f32[8,128]{1,0:T(8,128)}) custom-call(f32[512,512]{1,0:T(8,128)} %fusion.135.mid_ref, f32[512,128]{1,0:T(8,128)} %maximum_maximum_fusion.rest_ref, f32[512,512]{1,0:T(8,128)} %bitcast.220, f32[512,512]{1,0:T(8,128)} %bitcast.221, f32[512,128]{1,0:T(8,128)} %get-tuple-element.64.rest_first_ref, ...), custom_call_target="tpu_custom_call" | custom-call | tf_op jit(solution)/shard_map/pallas_call | solution.py:333
  136.4 1.3 slice.193
  138.4 1.1 slice_bitcast_fusion.2
  139.5 0.7 copy.127
  140.2 1.7 %copy.126 = f32[512,64]{0,1:T(8,128)} copy(f32[512,64]{1,0:T(8,128)} %bitcast.215) | data formatting | bytes 262144
  141.9 2.3 %fusion.24 = f32[32,32,128]{2,1,0:T(8,128)} fusion(f32[32,32,128]{2,1,0:T(8,128)S(1)} %copy-done.6, f32[32,32,128]{2,1,0:T(8,128)} %param.24, f32[]{:T(128)} %bitcast.26, f32[32,33,127]{2,1,0:T(8,128)S(1)} %slice.229, f32[32,33,1]{2,1,0:T(8,128)S(1)} %copy.115, f32[32,1,128]{2,1,0:T(1,128)S(1)} %slice_add_fusion.1), kind=kLoop, calls=%fused_computation.39 | loop fusion | flops 2228224 | bytes 2129924 | tf_op jit(solution)/shard_map/div | solution.py:145
  144.3 0.8 fusion.44
  145.0 1.0 copy.163
  (106 shorter events, 7.6 us)
Async XLA Ops:
  0.6 13.1 %copy-start.4 = (f32[32,32,128]{2,1,0:T(8,128)S(1)}, f32[32,32,128]{2,1,0:T(8,128)}, u32[]{:S(2)}) copy-start(f32[32,32,128]{2,1,0:T(8,128)} %param.19) | copy-start | bytes 1572868
  2.6 10.7 %collective-permute-start = (f32[32,1,160]{2,1,0:T(1,128)S(1)}, f32[32,1,160]{2,1,0:T(1,128)S(1)}, u32[]{:S(2)}, u32[]{:S(2)}) collective-permute-start(f32[32,1,160]{2,1,0:T(1,128)S(1)} %copy.103), channel_id=1, source_target_pairs={{4,0},{8,4},{12,8},{16,12},{20,16},{24,20},{28,24},{5,1},{9,5},{13... | collective-permute-start | bytes 61448 | tf_op jit(solution)/shard_map/ppermute | solution.py:26
  13.3 10.0 %copy-start.7 = (f32[512,64]{0,1:T(8,128)S(1)}, f32[512,64]{0,1:T(8,128)}, u32[]{:S(2)}) copy-start(f32[512,64]{0,1:T(8,128)} %param.21) | copy-start | bytes 393220
  14.2 5.4 %collective-permute-start.1 = (f32[32,42,1]{1,0,2:T(8,128)S(1)}, f32[32,42,1]{1,0,2:T(8,128)S(1)}, u32[]{:S(2)}, u32[]{:S(2)}) collective-permute-start(f32[32,42,1]{1,0,2:T(8,128)S(1)} %pad_maximum_fusion.7), channel_id=1, source_target_pairs={{1,0},{2,1},{3,2},{5,4},{6,5},{7,6},{9,8},{10,9},{11,10},{13,12},{... | collective-permute-start | bytes 16136 | tf_op jit(solution)/shard_map/ppermute | solution.py:26
  23.3 4.6 %copy-start.10 = (bf16[64,4096]{1,0:T(8,128)(2,1)}, bf16[64,4096]{1,0:T(8,128)(2,1)S(1)}, u32[]{:S(2)}) copy-start(bf16[64,4096]{1,0:T(8,128)(2,1)S(1)} %bitcast_dynamic-update-slice_fusion) | copy-start | bytes 1572868
  23.3 4.6 %copy-start.13 = (f32[1,512,512]{2,1,0:T(8,128)S(1)}, f32[1,512,512]{2,1,0:T(8,128)}, u32[]{:S(2)}) copy-start(f32[1,512,512]{2,1,0:T(8,128)} %param.22) | copy-start | bytes 3145732
  27.9 4.6 %copy-start = (bf16[512,4096]{0,1:T(8,128)(2,1)}, bf16[512,4096]{0,1:T(8,128)(2,1)S(1)}, u32[]{:S(2)}) copy-start(bf16[512,4096]{0,1:T(8,128)(2,1)S(1)} %get-tuple-element.50) | copy-start | bytes 12582916
  27.9 6.6 %copy-start.12 = (f32[3,512]{1,0:T(4,128)S(1)}, f32[3,512]{1,0:T(4,128)}, u32[]{:S(2)}) copy-start(f32[3,512]{1,0:T(4,128)} %param.23) | copy-start | bytes 18436
  32.6 2.0 %copy-start.2 = (bf16[512,4096]{0,1:T(8,128)(2,1)}, bf16[512,4096]{0,1:T(8,128)(2,1)S(1)}, u32[]{:S(2)}) copy-start(bf16[512,4096]{0,1:T(8,128)(2,1)S(1)} %get-tuple-element.52) | copy-start | bytes 12582916
  35.8 3.6 %collective-permute-start.4 = (f32[6,32,1]{2,1,0:T(8,128)S(1)}, f32[6,32,1]{2,1,0:T(8,128)S(1)}, u32[]{:S(2)}, u32[]{:S(2)}) collective-permute-start(f32[6,32,1]{2,1,0:T(8,128)S(1)} %pad_maximum_fusion.2), channel_id=1, source_target_pairs={{0,1},{1,2},{2,3},{4,5},{5,6},{6,7},{8,9},{9,10},{10,11},{12,13},{... | collective-permute-start | bytes 2312 | tf_op jit(solution)/shard_map/ppermute | solution.py:26
  39.4 6.3 %collective-permute-start.5 = (f32[3,32,1]{2,1,0:T(8,128)S(1)}, f32[3,32,1]{2,1,0:T(8,128)S(1)}, u32[]{:S(2)}, u32[]{:S(2)}) collective-permute-start(f32[3,32,1]{2,1,0:T(8,128)S(1)} %get-tuple-element.47), channel_id=1, source_target_pairs={{1,0},{2,1},{3,2},{5,4},{6,5},{7,6},{9,8},{10,9},{11,10},{13,12},{... | collective-permute-start | bytes 1160 | tf_op jit(solution)/shard_map/ppermute | solution.py:26
  41.4 4.4 %collective-permute-start.2 = (f32[6,1,128]{2,1,0:T(1,128)S(1)}, f32[6,1,128]{2,1,0:T(1,128)S(1)}, u32[]{:S(2)}, u32[]{:S(2)}) collective-permute-start(f32[6,1,128]{2,1,0:T(1,128)S(1)} %pad_maximum_fusion.9), channel_id=1, source_target_pairs={{0,4},{4,8},{8,12},{12,16},{16,20},{20,24},{24,28},{1,5},{5,9},{9,... | collective-permute-start | bytes 9224 | tf_op jit(solution)/shard_map/ppermute | solution.py:26
  45.7 14.3 %slice-start = ((s8[8388608]{0:T(1024)(128)(4,1)}), s8[4194304]{0:T(1024)(128)(4,1)S(1)}, s32[]{:S(2)}) async-start(s8[8388608]{0:T(1024)(128)(4,1)} %bitcast.229), calls=%async_computation | async-start | bytes 8388608
  45.9 4.6 %collective-permute-start.3 = (f32[3,1,128]{2,1,0:T(1,128)S(1)}, f32[3,1,128]{2,1,0:T(1,128)S(1)}, u32[]{:S(2)}, u32[]{:S(2)}) collective-permute-start(f32[3,1,128]{2,1,0:T(1,128)S(1)} %get-tuple-element.45), channel_id=1, source_target_pairs={{4,0},{8,4},{12,8},{16,12},{20,16},{24,20},{28,24},{5,1},{9,5},{13... | collective-permute-start | bytes 4616 | tf_op jit(solution)/shard_map/ppermute | solution.py:26
  50.9 5.8 %copy-start.11 = (bf16[3,4096]{1,0:T(4,128)(2,1)}, bf16[3,4096]{1,0:T(4,128)(2,1)S(1)}, u32[]{:S(2)}) copy-start(bf16[3,4096]{1,0:T(4,128)(2,1)S(1)} %fusion.53) | copy-start | bytes 73732
  50.9 5.8 %copy-start.1 = (bf16[512,4096]{0,1:T(8,128)(2,1)S(1)}, bf16[512,4096]{0,1:T(8,128)(2,1)}, u32[]{:S(2)}) copy-start(bf16[512,4096]{0,1:T(8,128)(2,1)} %copy-done) | copy-start | bytes 12582916
  50.9 9.1 %slice-start.1 = ((s8[8388608]{0:T(1024)(128)(4,1)}), s8[4194304]{0:T(1024)(128)(4,1)S(1)}, s32[]{:S(2)}) async-start(s8[8388608]{0:T(1024)(128)(4,1)} %bitcast.229), calls=%async_computation.1 | async-start | bytes 8388608
  63.6 2.0 %copy-start.3 = (bf16[512,4096]{0,1:T(8,128)(2,1)}, bf16[512,4096]{0,1:T(8,128)(2,1)S(1)}, u32[]{:S(2)}) copy-start(bf16[512,4096]{0,1:T(8,128)(2,1)S(1)} %fusion) | copy-start | bytes 12582916
  69.4 10.8 %collective-permute-start.6 = (f32[32,42,1]{1,0,2:T(8,128)S(1)}, f32[32,42,1]{1,0,2:T(8,128)S(1)}, u32[]{:S(2)}, u32[]{:S(2)}) collective-permute-start(f32[32,42,1]{1,0,2:T(8,128)S(1)} %pad_maximum_fusion.8), channel_id=1, source_target_pairs={{0,1},{1,2},{2,3},{4,5},{5,6},{6,7},{8,9},{9,10},{10,11},{12,13},{... | collective-permute-start | bytes 16136 | tf_op jit(solution)/shard_map/ppermute | solution.py:26
  81.2 5.2 %collective-permute-start.7 = (f32[32,1,160]{2,1,0:T(1,128)S(1)}, f32[32,1,160]{2,1,0:T(1,128)S(1)}, u32[]{:S(2)}, u32[]{:S(2)}) collective-permute-start(f32[32,1,160]{2,1,0:T(1,128)S(1)} %fusion.74), channel_id=1, source_target_pairs={{0,4},{4,8},{8,12},{12,16},{16,20},{20,24},{24,28},{1,5},{5,9},{9,... | collective-permute-start | bytes 61448 | tf_op jit(solution)/shard_map/ppermute | solution.py:26
  87.2 54.8 %copy-start.6 = (f32[32,32,128]{2,1,0:T(8,128)S(1)}, f32[32,32,128]{2,1,0:T(8,128)}, u32[]{:S(2)}) copy-start(f32[32,32,128]{2,1,0:T(8,128)} %param.25) | copy-start | bytes 1572868
  90.3 53.9 %copy-start.8 = (f32[32,8,32]{2,1,0:T(8,128)S(1)}, f32[32,8,32]{2,1,0:T(8,128)}, u32[]{:S(2)}) copy-start(f32[32,8,32]{2,1,0:T(8,128)} %param.27) | copy-start | bytes 98308
  90.3 53.9 %copy-start.9 = (f32[32,8,32]{2,1,0:T(8,128)S(1)}, f32[32,8,32]{2,1,0:T(8,128)}, u32[]{:S(2)}) copy-start(f32[32,8,32]{2,1,0:T(8,128)} %param.26) | copy-start | bytes 98308
  136.4 8.6 %copy-start.5 = (f32[512,512]{1,0:T(8,128)S(1)}, f32[512,512]{1,0:T(8,128)}, u32[]{:S(2)}) copy-start(f32[512,512]{1,0:T(8,128)} %get-tuple-element.10) | copy-start | bytes 3145732
where the time goes:
time: 147 us; the launch traced here: 146 us
  Pallas kernels  46 us (31%)
  matrix products  36.9 us (25%)
  starting transfers between devices  21.9 us (15%)
  local copies, waits for them, and re-layouts  21.1 us (14%)
  other arithmetic  7.81 us (5%)
  waiting for transfers between devices  7.59 us (5%)
  between operations  4.54 us (3%)
    pallas_call x1, Pallas kernels, decoder_steps(): pl.pallas_call(functools.partial(decoder_kernel, used), out_shape=(flat,...  46 us
    ppermute x8, starting transfers between devices, shifted(): return lax.ppermute(block, axis, route)  21.9 us
    unnamed x47, local copies, waits for them, and re-layouts  12 us
    dot_general x3, matrix products, contract_rows(): lax.dot_general(former, latter, (((0,), (0,)), ((), ())), preferred_eleme...  10.7 us
    dot_general x3, matrix products, matmul(): return jnp.dot(former, latter, preferred_element_type=jnp.float32)  10.4 us
    dot_general x3, matrix products, contract_cols(): lax.dot_general(former, latter, (((1,), (1,)), ((), ())), preferred_eleme...  10.4 us
    ppermute x8, waiting for transfers between devices, shifted(): return lax.ppermute(block, axis, route)  7.59 us
    div x2, other arithmetic, adam_step(): new_one / (1.0 - BETA_ONE ** ADAM_STEP)  3.06 us
  transfers between devices with their start and end apart: 8, of which 5 were waited for; matrix products, arithmetic and copies ran while one was open for 11% of the time, Pallas kernels for 0%

commit v1 on v0

v1 whole, which is shorter than its diff:
```python
import functools

import jax
import jax.numpy as jnp
from jax import lax
from jax.experimental import pallas as pl
from jax.experimental.pallas import tpu as pltpu
from jax.sharding import PartitionSpec as P

SUB = 4
RATIO = 4
ADAM_STEP = 10
BETA_ONE = 0.9
BETA_TWO = 0.99
ADAM_EPSILON = 1e-08
CLIP_RMS = 0.01
LOSS_VALUE = 0.25
MEAN_EPSILON = 1e-06

MESH = pl.DeviceIdType.MESH
LANES = 128
SUBLANES = 8
F32 = jnp.float32
BF16 = jnp.bfloat16


def clip_factor(total, entries):
    return jnp.minimum(1.0, CLIP_RMS / jnp.sqrt(total / entries + MEAN_EPSILON))


def adam_step(gradient, moment_one, moment_two, clip_scale):
    clipped = gradient * clip_scale
    new_one = BETA_ONE * moment_one + (1.0 - BETA_ONE) * clipped
    new_two = BETA_TWO * moment_two + (1.0 - BETA_TWO) * clipped * clipped
    return (
        new_one
        / (1.0 - BETA_ONE**ADAM_STEP)
        / (jnp.sqrt(new_two / (1.0 - BETA_TWO**ADAM_STEP)) + ADAM_EPSILON)
    )


def dot(former, latter, dims=((1,), (0,)), precision=None):
    return lax.dot_general(
        former, latter, (dims, ((), ())), preferred_element_type=F32, precision=precision
    )


def dot_t(former, latter, precision=None):
    return dot(former, latter, ((1,), (1,)), precision)


def gate(pre_act):
    sigmoid = 0.5 * jnp.tanh(0.5 * pre_act) + 0.5
    act = pre_act * sigmoid
    return act, sigmoid + act * (1.0 - sigmoid)


class Axis:
    def __init__(self, me, size, device):
        self.me, self.size, self.device = me, size, device

    def peer(self, step):
        return lax.rem(self.me + step, self.size)


def aligned(start):
    return pl.multiple_of(start, SUBLANES)


class Links:
    def __init__(self, send, recv):
        self.send, self.recv, self.used = send, recv, 0

    def take(self, count):
        first = self.used
        self.used += count
        return first

    def copy(self, source, target, device, slot):
        return pltpu.make_async_remote_copy(
            src_ref=source,
            dst_ref=target,
            send_sem=self.send.at[slot],
            recv_sem=self.recv.at[slot],
            device_id=device,
            device_id_type=MESH,
        )


class Scatter:
    def __init__(self, links, own, start, rows, axes, lands):
        self.links, self.own, self.axes, self.lands = links, own, axes, lands
        self.spans = [(start, rows)]
        for axis in axes:
            start, rows = self.spans[-1]
            part = rows // axis.size
            self.spans.append((start + axis.me * part, part))
        self.slots = [links.take(axis.size - 1) for axis in axes]

    def copies(self, stage):
        axis, land = self.axes[stage], self.lands[stage]
        start = self.spans[stage][0]
        part = self.spans[stage + 1][1]
        found = []
        for step in range(1, axis.size):
            peer = axis.peer(step)
            found.append(
                self.links.copy(
                    self.own.at[pl.ds(aligned(start + peer * part), part)],
                    land.at[step - 1],
                    axis.device(peer),
                    self.slots[stage] + step - 1,
                )
            )
        return found

    def start(self, stage):
        for copy in self.copies(stage):
            copy.start()

    def finish(self, stage):
        start, part = self.spans[stage + 1]
        span = pl.ds(aligned(start), part)
        for step, copy in enumerate(self.copies(stage)):
            copy.wait()
            self.own[span] += self.lands[stage][step]


class Gather:
    def __init__(self, scatter, full):
        self.scatter, self.full = scatter, full
        self.slots = [scatter.links.take(axis.size - 1) for axis in scatter.axes]

    def place(self):
        start, rows = self.scatter.spans[-1]
        span = pl.ds(aligned(start), rows)
        self.full[span] = self.scatter.own[span]

    def copies(self, stage):
        axis = self.scatter.axes[stage]
        start, rows = self.scatter.spans[stage + 1]
        block = self.full.at[pl.ds(aligned(start), rows)]
        return [
            self.scatter.links.copy(
                block, block, axis.device(axis.peer(step)), self.slots[stage] + step - 1
            )
            for step in range(1, axis.size)
        ]

    def start(self, stage):
        for copy in self.copies(stage):
            copy.start()

    def finish(self, stage):
        for copy in self.copies(stage):
            copy.wait()


def step_kernel(dims, *refs):
    refs = iter(refs)
    take = lambda count: [next(refs) for _ in range(count)]
    (offsets_ref,) = take(1)
    early_hbm = take(6)
    late_hbm = take(10)
    fine_out, coarse_out, in_out, mid_out, out_out = take(5)
    targets, fine, coarse, w_in, w_mid, w_out = early = take(6)
    late = take(10)
    (
        up_buf,
        cp_buf,
        below_buf,
        right_cp,
        diag_cp,
        coarse_s,
        across,
        across_c,
        b_in,
        b_in_t,
        b_mid,
        b_mid_t,
        b_out,
        b_out_t,
        feats,
        act_0,
        act_1,
        slope_0,
        slope_1,
        delta_1,
        pred,
        edge_send,
        edge_recv,
        cot_s,
        fgrad,
        down_buf,
        q_buf,
        above_buf,
        left_q,
        diag_q,
        fine_g,
        coarse_g,
        grad_in,
        grad_out,
        mid_away,
        mid_own,
        mid_pair,
        mid_full,
        rest_away,
        rest_own,
        rest_pair,
        rest_full,
        total_mine,
        total_land,
    ) = take(44)
    lands = take(12)
    load_sem, send_sem, recv_sem = take(3)

    rows_n, cols_n = lax.axis_size("row"), lax.axis_size("col")
    row, col = lax.axis_index("row"), lax.axis_index("col")
    CH, SR, SC, CR, CC, HID, OUT = (dims[k] for k in ("CH", "SR", "SC", "CR", "CC", "HID", "OUT"))
    S = SR * SC
    CHUNK = RATIO * SC
    CHUNKS = SR // RATIO

    core, plane = lax.rem(col, 2), lax.div(col, 2)
    x_at, z_at = lax.rem(row, 2), lax.div(row, 2)
    axis_core = Axis(core, 2, lambda p: (row, plane * 2 + p))
    axis_x = Axis(x_at, 2, lambda p: (z_at * 2 + p, col))
    axis_y = Axis(plane, cols_n // 2, lambda p: (row, p * 2 + core))
    axis_z = Axis(z_at, rows_n // 2, lambda p: (p * 2 + x_at, col))
    axes = (axis_core, axis_x, axis_y, axis_z)

    has_up, has_down = row > 0, row < rows_n - 1
    has_left, has_right = col > 0, col < cols_n - 1
    near = {
        "up": (has_up, (row - 1, col)),
        "down": (has_down, (row + 1, col)),
        "left": (has_left, (row, col - 1)),
        "right": (has_right, (row, col + 1)),
        "up_left": (jnp.logical_and(has_up, has_left), (row - 1, col - 1)),
        "down_right": (jnp.logical_and(has_down, has_right), (row + 1, col + 1)),
    }
    links = Links(send_sem, recv_sem)

    loads = [
        pltpu.make_async_copy(source, target, load_sem.at[place])
        for place, (source, target) in enumerate(zip(early_hbm + late_hbm, early + late))
    ]
    loads_early, loads_late = loads[:6], loads[6:]
    for place in (1, 2, 3, 4, 5, 0):
        loads_early[place].start()
    barrier = pltpu.get_barrier_semaphore()
    expected = sum(axis.size - 1 for axis in axes)
    for axis in axes:
        for step in range(1, axis.size):
            pl.semaphore_signal(
                barrier, inc=1, device_id=axis.device(axis.peer(step)), device_id_type=MESH
            )
    for there, device in near.values():
        expected = expected + there.astype(jnp.int32)

        @pl.when(there)
        def _():
            pl.semaphore_signal(barrier, inc=1, device_id=device, device_id_type=MESH)

    for load in loads_late:
        load.start()

    lane = lax.broadcasted_iota(jnp.int32, (CH, LANES), 1)
    lane_8 = lax.broadcasted_iota(jnp.int32, (SUBLANES, LANES), 1)
    off_y = offsets_ref[0, 0, 0].astype(F32) / SUB
    off_x = offsets_ref[0, 0, 1].astype(F32) / SUB

    def fine_row(r):
        return fine[pl.ds(r, CH, stride=SR), :]

    def roll(value, shift):
        return pltpu.roll(value, shift % LANES, 1)

    coarse_s[...] = jnp.zeros(coarse_s.shape, F32)
    up_buf[...] = jnp.zeros(up_buf.shape, F32)
    loads_early[1].wait()
    loads_early[2].wait()
    for r in range(CR):
        coarse_s[r, :, :CC] = coarse[pl.ds(r, CH, stride=CR), :]
    up_buf[0] = fine_row(0)
    up_buf[1] = coarse_s[0]
    packed = jnp.zeros((CH, LANES), F32)
    for r in range(SR):
        packed = jnp.where(lane == r, roll(fine_row(r), r), packed)
    for r in range(CR):
        packed = jnp.where(lane == SR + r, roll(coarse_s[r], SR + r), packed)
    cp_buf[...] = packed

    pl.semaphore_wait(barrier, expected)

    def halo(source, target, towards, back):
        slot = links.take(1)
        copy = links.copy(source, target, near[towards][1], slot)
        arriving = links.copy(source, target, near[back][1], slot)

        @pl.when(near[towards][0])
        def _():
            copy.start()

        def finish():
            @pl.when(near[towards][0])
            def _():
                copy.wait_send()

            @pl.when(near[back][0])
            def _():
                arriving.wait_recv()

        return finish

    waits = [
        halo(up_buf, below_buf, "up", "down"),
        halo(cp_buf, right_cp, "left", "right"),
        halo(cp_buf, diag_cp, "up_left", "down_right"),
    ]
    for target, back in ((below_buf, "down"), (right_cp, "right"), (diag_cp, "down_right")):

        @pl.when(jnp.logical_not(near[back][0]))
        def _():
            target[...] = jnp.zeros(target.shape, F32)

    loads_early[3].wait()
    loads_early[4].wait()
    loads_early[5].wait()
    b_in_t[...] = w_in[...].astype(BF16)
    b_in[...] = w_in[...].T.astype(BF16)
    b_mid[...] = w_mid[...].astype(BF16)
    b_mid_t[...] = w_mid[...].T.astype(BF16)
    padded_out = jnp.concatenate([w_out[...], jnp.zeros((SUBLANES - OUT, HID), F32)], axis=0)
    b_out[...] = padded_out.astype(BF16)
    b_out_t[...] = padded_out.T.astype(BF16)
    cot_s[...] = jnp.zeros(cot_s.shape, F32)
    vertex = lax.broadcasted_iota(jnp.int32, (LANES, LANES), 0)
    sample = lax.broadcasted_iota(jnp.int32, (LANES, LANES), 1)
    base = lax.div(sample, RATIO)
    fraction = (lax.rem(sample, RATIO).astype(F32) + off_x) / RATIO
    table = jnp.where(vertex == base, 1.0 - fraction, 0.0) + jnp.where(
        vertex == base + 1, fraction, 0.0
    )
    for wait in waits:
        wait()

    for r in range(SR + 1):
        value = fine_row(r) if r < SR else below_buf[0]
        edge = roll(right_cp[...], LANES - 1 - r) if r < SR else roll(diag_cp[...], LANES - 1)
        shifted = jnp.where(lane == LANES - 1, edge, roll(value, LANES - 1))
        across[r] = (1.0 - off_x) * value + off_x * shifted
    for r in range(CR + 1):
        value = coarse_s[r] if r < CR else below_buf[1]
        edge = roll(right_cp[...], CC - SR - r) if r < CR else roll(diag_cp[...], CC - SR)
        coarse_s[r] = jnp.where(lane == CC, edge, value)
    across_c[...] = dot(
        coarse_s[...].reshape((CR + 1) * CH, LANES), table, precision=lax.Precision.HIGHEST
    ).reshape(CR + 1, CH, LANES)

    def chunk_span(c):
        return pl.ds(pl.multiple_of(c * CHUNK, CHUNK), CHUNK)

    @pl.loop(0, CHUNKS)
    def _(c):
        for k in range(RATIO):
            i = c * RATIO + k
            span = pl.ds(pl.multiple_of(i * SC, SC), SC)
            part = (k + off_y) / RATIO
            feats[:CH, span] = ((1.0 - off_y) * across[i] + off_y * across[i + 1]).astype(BF16)
            feats[CH:, span] = ((1.0 - part) * across_c[c] + part * across_c[c + 1]).astype(BF16)
        span = chunk_span(c)
        act, slope = gate(dot(b_in[...], feats[:, span]))
        act_0[:, span] = act.astype(BF16)
        slope_0[:, span] = slope
        act, slope = gate(dot(b_mid[...], act_0[:, span]))
        act_1[:, span] = act.astype(BF16)
        slope_1[:, span] = slope
        colours = dot(b_out[...], act_1[:, span])
        for k in range(RATIO):
            pred[c * RATIO + k + 1] = colours[:, k * SC : (k + 1) * SC]

    loads_early[0].wait()

    def target_row(kind, r):
        found = targets[pl.ds(kind * OUT * SR + r, OUT, stride=SR), :]
        return jnp.concatenate([found, jnp.zeros((SUBLANES - OUT, LANES), F32)], axis=0)

    first_col = jnp.zeros((SUBLANES, LANES), F32)
    last_col = jnp.zeros((SUBLANES, LANES), F32)
    last_aim = jnp.zeros((SUBLANES, LANES), F32)
    for r in range(SR):
        first_col = jnp.where(lane_8 == r, roll(pred[r + 1], r), first_col)
        last_col = jnp.where(lane_8 == r, roll(pred[r + 1], r + 1), last_col)
        last_aim = jnp.where(lane_8 == r, roll(target_row(2, r), r + 1), last_aim)
    edge_send[0, 0] = pred[1]
    edge_send[1, 0] = first_col
    edge_send[2, 0] = pred[SR]
    edge_send[2, 1] = target_row(1, SR - 1)
    edge_send[3, 0] = last_col
    edge_send[3, 1] = last_aim
    waits = [
        halo(edge_send.at[0, 0], edge_recv.at[0, 0], "up", "down"),
        halo(edge_send.at[1, 0], edge_recv.at[1, 0], "left", "right"),
        halo(edge_send.at[2], edge_recv.at[2], "down", "up"),
        halo(edge_send.at[3], edge_recv.at[3], "right", "left"),
    ]
    for place, back in enumerate(("down", "right", "up", "left")):

        @pl.when(jnp.logical_not(near[back][0]))
        def _():
            edge_recv[place] = jnp.zeros(edge_recv.shape[1:], F32)

    for wait in waits:
        wait()

    pred[SR + 1] = edge_recv[0, 0]
    prior = jnp.where(has_up, (pred[1] - edge_recv[2, 0]) - edge_recv[2, 1], 0.0)
    for r in range(SR):
        here = pred[r + 1]
        row_error = (pred[r + 2] - here) - target_row(1, r)
        if r == SR - 1:
            row_error = jnp.where(has_down, row_error, 0.0)
        beside = jnp.where(lane_8 == LANES - 1, roll(edge_recv[1, 0], LANES - 1 - r), roll(here, -1))
        col_error = (beside - here) - target_row(2, r)
        closed = jnp.logical_and(lane_8 == LANES - 1, jnp.logical_not(has_right))
        col_error = jnp.where(closed, 0.0, col_error)
        before = (here - roll(edge_recv[3, 0], -r)) - roll(edge_recv[3, 1], -r)
        before = jnp.where(has_left, before, 0.0)
        col_prior = jnp.where(lane_8 == 0, before, roll(col_error, 1))
        value_error = here - target_row(0, r)
        cot = (
            2.0 * LOSS_VALUE * value_error
            + 2.0 * (prior - row_error)
            + 2.0 * (col_prior - col_error)
        )
        kept = lax.broadcasted_iota(jnp.int32, (SUBLANES, LANES), 0) < OUT
        cot_s[:, r * SC : (r + 1) * SC] = jnp.where(kept, cot, 0.0)
        prior = row_error

    grad_out[...] = jnp.zeros(grad_out.shape, F32)

    @pl.loop(0, CHUNKS)
    def _(c):
        span = chunk_span(c)
        cot = cot_s[:, span].astype(BF16)
        delta_1[:, span] = (dot(b_out_t[...], cot) * slope_1[:, span]).astype(BF16)
        grad_out[...] += dot_t(cot, act_1[:, span])

    half = HID // 2
    mid_rows = HID * half // LANES
    rest_rows = rest_own.shape[0]

    def mid_half(which, target):
        lower = act_0[pl.ds(pl.multiple_of(which * half, half), half), :]
        block = dot_t(delta_1[...], lower)
        for part in range(half // LANES):
            target[part * HID : (part + 1) * HID, :] = block[:, part * LANES : (part + 1) * LANES]

    partner = axis_core.device(1 - core)
    mid_half(1 - core, mid_away)
    pair_mid = links.copy(mid_away, mid_pair, partner, links.take(1))
    pair_mid.start()
    mid_half(core, mid_own)
    orders = ((axis_x, axis_y, axis_z), (axis_y, axis_x, axis_z))
    mids = [
        Scatter(links, mid_own, k * (mid_rows // 2), mid_rows // 2, orders[k], lands[k * 3 : k * 3 + 3])
        for k in range(2)
    ]
    rests = [
        Scatter(
            links,
            rest_own,
            k * (rest_rows // 2),
            rest_rows // 2,
            orders[k],
            lands[6 + k * 3 : 9 + k * 3],
        )
        for k in range(2)
    ]
    pair_mid.wait()
    mid_own[...] += mid_pair[...]
    for scatter in mids:
        scatter.start(0)

    grad_in[...] = jnp.zeros(grad_in.shape, F32)

    def lower_chunks(first, last):
        @pl.loop(first, last)
        def _(c):
            span = chunk_span(c)
            delta = (dot(b_mid_t[...], delta_1[:, span]) * slope_0[:, span]).astype(BF16)
            grad_in[...] += dot_t(feats[:, span], delta)
            spread = dot(b_in_t[...], delta)
            for k in range(RATIO):
                fgrad[c * RATIO + k] = spread[:, k * SC : (k + 1) * SC]

    lower_chunks(0, CHUNKS // 2)
    for scatter in mids:
        scatter.finish(0)
    for scatter in mids:
        scatter.start(1)
    lower_chunks(CHUNKS // 2, CHUNKS)
    for scatter in mids:
        scatter.finish(1)
    for scatter in mids:
        scatter.start(2)

    blocks = HID // LANES
    inputs = 2 * CH
    block_rows = rest_rows // (blocks // 2)

    def rest_half(which, target):
        for part in range(blocks // 2):
            for choice in range(2):

                @pl.when(which == choice)
                def _():
                    at = (choice * (blocks // 2) + part) * LANES
                    start = part * block_rows
                    target[start : start + inputs, :] = grad_in[:, at : at + LANES]
                    target[start + inputs : start + inputs + SUBLANES, :] = grad_out[:, at : at + LANES]
                    used = inputs + SUBLANES
                    target[start + used : start + block_rows, :] = jnp.zeros(
                        (block_rows - used, LANES), F32
                    )

    rest_half(1 - core, rest_away)
    pair_rest = links.copy(rest_away, rest_pair, partner, links.take(1))
    pair_rest.start()
    rest_half(core, rest_own)

    last = SR
    bottom = None
    packed = jnp.zeros((CH, LANES), F32)
    zero = jnp.zeros((CH, LANES), F32)
    for r in range(SR + 1):
        value = zero
        if r < SR:
            value = (1.0 - off_y) * fgrad[r, :CH]
        if r > 0:
            value = value + off_y * fgrad[r - 1, :CH]
        moved = off_x * roll(value, 1)
        out = (1.0 - off_x) * value + jnp.where(lane == 0, 0.0, moved)
        at = r if r < SR else SR + CR
        packed = jnp.where(lane == at, roll(moved, at), packed)
        if r < SR:
            fine_g[r] = out
        else:
            down_buf[0] = out
    for j in range(CR + 1):
        value = zero
        for k in range(RATIO):
            part = (k + off_y) / RATIO
            if j < CR:
                value = value + (1.0 - part) * fgrad[j * RATIO + k, CH:]
            if j > 0:
                value = value + part * fgrad[(j - 1) * RATIO + k, CH:]
        coarse_s[j] = value
    spread = dot_t(
        coarse_s[...].reshape((CR + 1) * CH, LANES), table, precision=lax.Precision.HIGHEST
    ).reshape(CR + 1, CH, LANES)
    for j in range(CR + 1):
        value = spread[j]
        at = SR + j if j < CR else SR + CR + 1
        packed = jnp.where(lane == at, roll(value, at - CC), packed)
        value = jnp.where(lane < CC, value, 0.0)
        if j < CR:
            coarse_g[j] = value
        else:
            down_buf[1] = value
    q_buf[...] = packed
    waits = [
        halo(down_buf, above_buf, "down", "up"),
        halo(q_buf, left_q, "right", "left"),
        halo(q_buf, diag_q, "down_right", "up_left"),
    ]
    for target, back in ((above_buf, "up"), (left_q, "left"), (diag_q, "up_left")):

        @pl.when(jnp.logical_not(near[back][0]))
        def _():
            target[...] = jnp.zeros(target.shape, F32)

    pair_rest.wait()
    rest_own[...] += rest_pair[...]
    for scatter in rests:
        scatter.start(0)

    for wait in waits:
        wait()
    fine_g[0] += above_buf[0] + jnp.where(lane == 0, roll(diag_q[...], -(SR + CR)), 0.0)
    coarse_g[0] += above_buf[1] + jnp.where(lane == 0, roll(diag_q[...], -(SR + CR + 1)), 0.0)
    squares = jnp.zeros((CH, LANES), F32)
    for r in range(SR):
        value = fine_g[r] + jnp.where(lane == 0, roll(left_q[...], -r), 0.0)
        fine_g[r] = value
        squares += value * value
    for j in range(CR):
        value = coarse_g[j] + jnp.where(lane == 0, roll(left_q[...], -(SR + j)), 0.0)
        coarse_g[j] = value
        squares += value * value
    total = squares[:SUBLANES]
    for part in range(1, CH // SUBLANES):
        total = total + squares[part * SUBLANES : (part + 1) * SUBLANES]
    total_mine[0] = total

    def total_copies(stage):
        axis = axes[stage]
        return [
            links.copy(
                total_mine.at[stage],
                total_land.at[total_slots[stage] - total_slots[0] + step - 1],
                axis.device(axis.peer(step)),
                total_slots[stage] + step - 1,
            )
            for step in range(1, axis.size)
        ]

    total_slots = [links.take(axis.size - 1) for axis in axes]

    def total_start(stage):
        for copy in total_copies(stage):
            copy.start()

    def total_finish(stage):
        found = total_mine[stage]
        for step, copy in enumerate(total_copies(stage)):
            copy.wait()
            found = found + total_land[total_slots[stage] - total_slots[0] + step]
        total_mine[stage + 1] = found

    total_start(0)
    gathers = [Gather(scatter, full) for scatter, full in zip(mids, (mid_full.at[core],) * 2)]
    gathers += [Gather(scatter, full) for scatter, full in zip(rests, (rest_full.at[core],) * 2)]
    for scatter in rests:
        scatter.finish(0)
    for scatter in rests:
        scatter.start(1)
    total_finish(0)
    total_start(1)
    for scatter, gather in zip(mids, gathers):
        scatter.finish(2)
        gather.place()
        gather.start(2)
    for scatter in rests:
        scatter.finish(1)
    for scatter in rests:
        scatter.start(2)
    total_finish(1)
    total_start(2)
    for scatter, gather in zip(rests, gathers[2:]):
        scatter.finish(2)
        gather.place()
        gather.start(2)
    total_finish(2)
    total_start(3)
    for gather in gathers:
        gather.finish(2)
        gather.start(1)
    total_finish(3)

    for load in loads_late:
        load.wait()
    fine_first, fine_second, coarse_first, coarse_second = late[:4]
    in_first, in_second, mid_first, mid_second, out_first, out_second = late[4:]
    entries = CH * (SR * SC + CR * CC) * rows_n * cols_n
    grid_scale = clip_factor(jnp.sum(total_mine[4], keepdims=True), entries)
    for r in range(SR):
        span = pl.ds(r, CH, stride=SR)
        fine_out[span, :] = adam_step(fine_g[r], fine_first[span, :], fine_second[span, :], grid_scale)
    for j in range(CR):
        span = pl.ds(j, CH, stride=CR)
        coarse_out[span, :] = adam_step(
            coarse_g[j, :, :CC], coarse_first[span, :], coarse_second[span, :], grid_scale
        )

    for gather in gathers:
        gather.finish(1)
        gather.start(0)
    for gather in gathers:
        gather.finish(0)
    last_mid = links.copy(mid_full.at[core], mid_full.at[core], partner, links.take(1))
    last_rest = links.copy(rest_full.at[core], rest_full.at[core], partner, links.take(1))
    last_mid.start()
    last_rest.start()
    last_mid.wait()
    last_rest.wait()

    squares = jnp.zeros((SUBLANES, LANES), F32)
    for which in range(2):
        for start in range(0, mid_rows, HID):
            value = mid_full[which, start : start + HID, :]
            value = (value * value).reshape(HID // SUBLANES, SUBLANES, LANES)
            squares += jnp.sum(value, axis=0)
        for part in range(blocks // 2):
            start = part * block_rows
            value = rest_full[which, start : start + inputs + SUBLANES, :]
            value = (value * value).reshape(inputs // SUBLANES + 1, SUBLANES, LANES)
            squares += jnp.sum(value, axis=0)
    scale = clip_factor(jnp.sum(squares, keepdims=True), HID * (HID + inputs + OUT))
    for which in range(2):
        for part in range(blocks // 2):
            at = (which * (blocks // 2) + part) * LANES
            lanes = slice(at, at + LANES)
            mid_out[:, lanes] = adam_step(
                mid_full[which, part * HID : (part + 1) * HID, :],
                mid_first[:, lanes],
                mid_second[:, lanes],
                scale,
            )
            start = part * block_rows
            in_out[:, lanes] = adam_step(
                rest_full[which, start : start + inputs, :],
                in_first[:, lanes],
                in_second[:, lanes],
                scale,
            )
            out_out[:, lanes] = adam_step(
                rest_full[which, start + inputs : start + inputs + OUT, :],
                out_first[:, lanes],
                out_second[:, lanes],
                scale,
            )
    assert links.used <= dims["COPIES"]


def shards(
    offsets,
    targets,
    grid_fine,
    grid_coarse,
    weight_in,
    weight_mid,
    weight_out,
    fine_first,
    fine_second,
    coarse_first,
    coarse_second,
    in_first,
    in_second,
    mid_first,
    mid_second,
    out_first,
    out_second,
):
    CH, SR, SC = grid_fine.shape
    CR, CC = grid_coarse.shape[1:]
    HID = weight_in.shape[0]
    OUT = weight_out.shape[0]
    S = SR * SC
    rows_n, cols_n = lax.axis_size("row"), lax.axis_size("col")
    sizes_x, sizes_y, sizes_z = 2, cols_n // 2, rows_n // 2
    peers = (sizes_x - 1) + (sizes_y - 1) + (sizes_z - 1)
    copies = 8 * peers + peers + 1 + 4 + 10
    owners = sizes_x * sizes_y * sizes_z
    half_blocks = HID // LANES // 2
    block_rows = -(-(2 * CH + SUBLANES) // SUBLANES) * SUBLANES
    rest_rows = half_blocks * block_rows
    rest_rows = -(-rest_rows // (owners * SUBLANES * half_blocks)) * owners * SUBLANES * half_blocks
    mid_rows = HID * HID // 2 // LANES
    dims = dict(CH=CH, SR=SR, SC=SC, CR=CR, CC=CC, HID=HID, OUT=OUT, COPIES=copies)

    flat = lambda grid: grid.reshape(-1, grid.shape[-1])
    early = (
        flat(targets),
        flat(grid_fine),
        flat(grid_coarse),
        weight_in.T,
        weight_mid[0],
        weight_out,
    )
    late = (
        flat(fine_first),
        flat(fine_second),
        flat(coarse_first),
        flat(coarse_second),
        in_first.T,
        in_second.T,
        mid_first[0],
        mid_second[0],
        out_first,
        out_second,
    )
    vmem = lambda *shape: pltpu.VMEM(shape, F32)
    low = lambda *shape: pltpu.VMEM(shape, BF16)

    def landing(rows, sizes):
        found = []
        for size in sizes:
            rows = rows // size
            found.append(vmem(max(size - 1, 1), rows, LANES))
        return found

    orders = ((sizes_x, sizes_y, sizes_z), (sizes_y, sizes_x, sizes_z))
    scratch = [pltpu.VMEM(a.shape, F32) for a in early + late]
    scratch += [
        vmem(2, CH, LANES),
        vmem(CH, LANES),
        vmem(2, CH, LANES),
        vmem(CH, LANES),
        vmem(CH, LANES),
        vmem(CR + 1, CH, LANES),
        vmem(SR + 1, CH, LANES),
        vmem(CR + 1, CH, LANES),
        low(HID, 2 * CH),
        low(2 * CH, HID),
        low(HID, HID),
        low(HID, HID),
        low(SUBLANES, HID),
        low(HID, SUBLANES),
        low(2 * CH, S),
        low(HID, S),
        low(HID, S),
        vmem(HID, S),
        vmem(HID, S),
        low(HID, S),
        vmem(SR + 2, SUBLANES, LANES),
        vmem(4, 2, SUBLANES, LANES),
        vmem(4, 2, SUBLANES, LANES),
        vmem(SUBLANES, S),
        vmem(SR, 2 * CH, LANES),
        vmem(2, CH, LANES),
        vmem(CH, LANES),
        vmem(2, CH, LANES),
        vmem(CH, LANES),
        vmem(CH, LANES),
        vmem(SR, CH, LANES),
        vmem(CR, CH, LANES),
        vmem(2 * CH, HID),
        vmem(SUBLANES, HID),
        vmem(mid_rows, LANES),
        vmem(mid_rows, LANES),
        vmem(mid_rows, LANES),
        vmem(2, mid_rows, LANES),
        vmem(rest_rows, LANES),
        vmem(rest_rows, LANES),
        vmem(rest_rows, LANES),
        vmem(2, rest_rows, LANES),
        vmem(5, SUBLANES, LANES),
        vmem(peers + 1, SUBLANES, LANES),
    ]
    for order in orders:
        scratch += landing(mid_rows // 2, order)
    for order in orders:
        scratch += landing(rest_rows // 2, order)
    scratch += [
        pltpu.SemaphoreType.DMA((len(early) + len(late),)),
        pltpu.SemaphoreType.DMA((copies,)),
        pltpu.SemaphoreType.DMA((copies,)),
    ]
    outs = (
        (CH * SR, SC),
        (CH * CR, CC),
        (2 * CH, HID),
        (HID, HID),
        (OUT, HID),
    )
    fine_step, coarse_step, in_step, mid_step, out_step = pl.pallas_call(
        functools.partial(step_kernel, dims),
        out_shape=[jax.ShapeDtypeStruct(shape, F32) for shape in outs],
        in_specs=[pl.BlockSpec(memory_space=pltpu.SMEM)]
        + [pl.BlockSpec(memory_space=pl.ANY)] * (len(early) + len(late)),
        out_specs=[pl.BlockSpec(memory_space=pltpu.VMEM)] * len(outs),
        scratch_shapes=scratch,
        compiler_params=pltpu.CompilerParams(
            collective_id=0, has_side_effects=True, vmem_limit_bytes=66 * 1024 * 1000
        ),
    )(offsets, *early, *late)
    return (
        fine_step.reshape(grid_fine.shape),
        coarse_step.reshape(grid_coarse.shape),
        in_step.T,
        mid_step[None],
        out_step,
    )


def solution(mesh):
    tile, copied = P(None, "row", "col"), P()
    placed = (P("row", "col", None), P(None, None, "row", "col"), tile, tile)
    placed += (copied,) * 3 + (tile,) * 4 + (copied,) * 6
    return jax.shard_map(
        shards,
        mesh=mesh,
        in_specs=placed,
        out_specs=(tile, tile, copied, copied, copied),
        check_vma=False,
    )
```

time: 147 us -> 70.8 us (0.48)
  the two profiles are of different devices: /device:TPU:27 before, /device:TPU:0 now
where the time goes in v1:
time: 70.8 us; the launch traced here: 70.7 us
  Pallas kernels  64.2 us (91%)
  local copies, waits for them, and re-layouts  5.79 us (8%)
    pallas_call x1, Pallas kernels, shards(): pl.pallas_call(functools.partial(step_kernel, dims), out_shape=[jax.Shape...  64.2 us
    unnamed x11, local copies, waits for them, and re-layouts  5.79 us

profile of v1, /device:TPU:0, one launch (start us, length us, event | category | flops | bytes accessed | tf_op | source)
XLA Modules:
  0.0 70.7 jit_solution(13946191548773460960)
XLA Ops:
  0.6 64.2 %shard_map.200 = (f32[1024,128]{1,0:T(8,128)}, f32[256,32]{1,0:T(8,128)}, f32[64,512]{1,0:T(8,128)}, f32[512,512]{1,0:T(8,128)}, f32[3,512]{1,0:T(4,128)}) custom-call(s32[1,1,2]{2,1,0:T(1,128)} %refs_0_.1, f32[288,128]{1,0:T(8,128)} %bitcast.25, f32[1024,128]{1,0:T(8,128)} %bitcast.21, f32[256,32]{1,0:T(8,128)} %bitcast.26, f32[64,512]{1,0:T(8,128)} %bitcast.27, ...), custom_call_target="tpu_custom_call" | custom-call | tf_op jit(solution)/shard_map/pallas_call | solution.py:858
  64.9 0.0 copy-start
  64.9 2.0 %copy.27 = f32[32,32,128]{2,1,0:T(8,128)} copy(f32[32,32,128]{2,1,0:T(8,128)} %bitcast.24) | data formatting | bytes 1048576
  66.8 0.0 copy-start.1
  66.8 1.6 %copy.28 = f32[32,8,32]{2,1,0:T(8,128)} copy(f32[32,8,32]{2,1,0:T(8,128)} %bitcast.33) | data formatting | bytes 65536
  68.4 0.0 copy-done.1
  68.4 0.7 copy.29
  69.1 0.0 copy-done
  69.1 0.0 copy-start.2
  69.1 1.0 %copy.30 = f32[1,512,512]{2,1,0:T(8,128)} copy(f32[1,512,512]{2,1,0:T(8,128)S(1)} %bitcast.17) | data formatting | bytes 2097152
  70.1 0.0 copy-done.2
  70.1 0.6 copy.31
Async XLA Ops:
  64.9 4.2 %copy-start = (f32[512,512]{1,0:T(8,128)S(1)}, f32[512,512]{1,0:T(8,128)}, u32[]{:S(2)}) copy-start(f32[512,512]{1,0:T(8,128)} %get-tuple-element.13) | copy-start | bytes 3145732
  66.8 1.6 %copy-start.1 = (f32[64,512]{1,0:T(8,128)S(1)}, f32[64,512]{1,0:T(8,128)}, u32[]{:S(2)}) copy-start(f32[64,512]{1,0:T(8,128)} %get-tuple-element.12) | copy-start | bytes 393220
  69.1 1.0 %copy-start.2 = (f32[3,512]{1,0:T(4,128)S(1)}, f32[3,512]{1,0:T(4,128)}, u32[]{:S(2)}) copy-start(f32[3,512]{1,0:T(4,128)} %get-tuple-element.24) | copy-start | bytes 18436

commit v2 on v1

v2 whole, which is shorter than its diff:
```python
import functools

import jax
import jax.numpy as jnp
from jax import lax
from jax.experimental import pallas as pl
from jax.experimental.pallas import tpu as pltpu
from jax.sharding import PartitionSpec as P

SUB = 4
RATIO = 4
ADAM_STEP = 10
BETA_ONE = 0.9
BETA_TWO = 0.99
ADAM_EPSILON = 1e-08
CLIP_RMS = 0.01
LOSS_VALUE = 0.25
MEAN_EPSILON = 1e-06

MESH = pl.DeviceIdType.MESH
LANES = 128
SUBLANES = 8
F32 = jnp.float32
BF16 = jnp.bfloat16


def clip_factor(total, entries):
    return jnp.minimum(1.0, CLIP_RMS / jnp.sqrt(total / entries + MEAN_EPSILON))


def adam_step(gradient, moment_one, moment_two, clip_scale):
    rise_one = 1.0 / (1.0 - BETA_ONE**ADAM_STEP)
    rise_two = 1.0 / (1.0 - BETA_TWO**ADAM_STEP)
    new_one = (BETA_ONE * rise_one) * moment_one + gradient * (
        clip_scale * ((1.0 - BETA_ONE) * rise_one)
    )
    root = gradient * (clip_scale * ((1.0 - BETA_TWO) * rise_two) ** 0.5)
    new_two = (BETA_TWO * rise_two) * moment_two + root * root
    return new_one / (jnp.sqrt(new_two) + ADAM_EPSILON)


def dot(former, latter, dims=((1,), (0,)), precision=None):
    return lax.dot_general(
        former, latter, (dims, ((), ())), preferred_element_type=F32, precision=precision
    )


def dot_t(former, latter, precision=None):
    return dot(former, latter, ((1,), (1,)), precision)


def gate(pre_act):
    sigmoid = 0.5 * jnp.tanh(0.5 * pre_act) + 0.5
    act = pre_act * sigmoid
    return act, sigmoid + act * (1.0 - sigmoid)


class Axis:
    def __init__(self, me, size, device):
        self.me, self.size, self.device = me, size, device

    def peer(self, step):
        return lax.rem(self.me + step, self.size)


def aligned(start):
    return pl.multiple_of(start, SUBLANES)


class Links:
    def __init__(self, send, recv):
        self.send, self.recv, self.used = send, recv, 0

    def take(self, count):
        first = self.used
        self.used += count
        return first

    def copy(self, source, target, device, slot):
        return pltpu.make_async_remote_copy(
            src_ref=source,
            dst_ref=target,
            send_sem=self.send.at[slot],
            recv_sem=self.recv.at[slot],
            device_id=device,
            device_id_type=MESH,
        )


class Scatter:
    def __init__(self, links, own, start, rows, axes, lands):
        self.links, self.own, self.axes, self.lands = links, own, axes, lands
        self.spans = [(start, rows)]
        for axis in axes:
            start, rows = self.spans[-1]
            part = rows // axis.size
            self.spans.append((start + axis.me * part, part))
        self.slots = [links.take(axis.size - 1) for axis in axes]

    def copies(self, stage):
        axis, land = self.axes[stage], self.lands[stage]
        start = self.spans[stage][0]
        part = self.spans[stage + 1][1]
        found = []
        for step in range(1, axis.size):
            peer = axis.peer(step)
            found.append(
                self.links.copy(
                    self.own.at[pl.ds(aligned(start + peer * part), part)],
                    land.at[step - 1],
                    axis.device(peer),
                    self.slots[stage] + step - 1,
                )
            )
        return found

    def start(self, stage):
        for copy in self.copies(stage):
            copy.start()

    def finish(self, stage):
        start, part = self.spans[stage + 1]
        span = pl.ds(aligned(start), part)
        for step, copy in enumerate(self.copies(stage)):
            copy.wait()
            self.own[span] += self.lands[stage][step]


class Gather:
    def __init__(self, scatter, full):
        self.scatter, self.full = scatter, full
        self.slots = [scatter.links.take(axis.size - 1) for axis in scatter.axes]

    def place(self):
        start, rows = self.scatter.spans[-1]
        span = pl.ds(aligned(start), rows)
        self.full[span] = self.scatter.own[span]

    def copies(self, stage):
        axis = self.scatter.axes[stage]
        start, rows = self.scatter.spans[stage + 1]
        block = self.full.at[pl.ds(aligned(start), rows)]
        return [
            self.scatter.links.copy(
                block, block, axis.device(axis.peer(step)), self.slots[stage] + step - 1
            )
            for step in range(1, axis.size)
        ]

    def start(self, stage):
        for copy in self.copies(stage):
            copy.start()

    def finish(self, stage):
        for copy in self.copies(stage):
            copy.wait()


class Crowd:
    def __init__(self, links, axis, source, target):
        self.links, self.axis, self.slot = links, axis, links.take(1)
        self.source, self.target = source, target

    def start(self):
        @pl.loop(1, self.axis.size)
        def _(step):
            peer = self.axis.peer(step)
            self.links.copy(
                self.source(peer), self.target(self.axis.me), self.axis.device(peer), self.slot
            ).start()

    def wait(self, sent, landed):
        if self.axis.size > 1:
            device = self.axis.device(self.axis.peer(1))
            self.links.copy(sent, sent, device, self.slot).wait_send()
            self.links.copy(landed, landed, device, self.slot).wait_recv()


class Total:
    def __init__(self, links, mine, lands, axes):
        self.mine, self.lands, self.axes = mine, lands, axes
        self.crowds = [
            Crowd(links, axis, lambda peer: mine, lambda me, land=land: land.at[me])
            for axis, land in zip(axes, lands)
        ]
        self.stage = 0

    def start(self):
        self.lands[self.stage][self.axes[self.stage].me] = self.mine[...]
        self.crowds[self.stage].start()

    def finish(self):
        land, count = self.lands[self.stage], self.axes[self.stage].size
        span = land.at[pl.ds(0, max(count - 1, 1))]
        self.crowds[self.stage].wait(span, span)
        total = land[0]
        for place in range(1, count):
            total = total + land[place]
        self.stage += 1
        if self.stage < len(self.axes):
            self.mine[...] = total
            self.start()
        return total


def step_kernel(dims, *refs):
    refs = iter(refs)
    take = lambda count: [next(refs) for _ in range(count)]
    (offsets_hbm,) = take(1)
    early_hbm = take(6)
    late_hbm = take(4)
    kept_hbm = take(6)
    fine_out, coarse_out, mid_full, in_full, out_full = take(5)
    kept = take(6)
    (offsets_ref,) = take(1)
    targets, fine, coarse, w_in, w_mid, w_out = early = take(6)
    late = take(4)
    (
        up_buf,
        cp_buf,
        below_buf,
        right_cp,
        diag_cp,
        coarse_s,
        across,
        across_c,
        b_in,
        b_in_t,
        b_mid,
        b_mid_t,
        b_out,
        b_out_t,
        feats,
        act_0,
        act_1,
        slope_0,
        slope_1,
        delta_1,
        pred,
        edge_send,
        edge_recv,
        col_send,
        col_recv,
        cot_s,
        fgrad,
        down_buf,
        q_buf,
        above_buf,
        left_q,
        diag_q,
        fine_g,
        coarse_g,
        grad_in,
        grad_out,
        mid_away,
        mid_own,
        mid_pair,
        in_away,
        in_own,
        in_pair,
        in_land,
        total_mine,
    ) = take(44)
    out_lands = take(4)
    total_lands = take(2)
    lands = take(12)
    load_sem, send_sem, recv_sem, know_sem = take(4)

    rows_n, cols_n = lax.axis_size("row"), lax.axis_size("col")
    row, col = lax.axis_index("row"), lax.axis_index("col")
    CH, SR, SC, CR, CC, HID, OUT = (dims[k] for k in ("CH", "SR", "SC", "CR", "CC", "HID", "OUT"))
    S = SR * SC
    CHUNK = dims["GROUP"] * SC
    CHUNKS = S // CHUNK
    GROUP = dims["GROUP"]

    core, plane = lax.rem(col, 2), lax.div(col, 2)
    x_at, z_at = lax.rem(row, 2), lax.div(row, 2)
    axis_core = Axis(core, 2, lambda p: (row, plane * 2 + p))
    axis_x = Axis(x_at, 2, lambda p: (z_at * 2 + p, col))
    axis_y = Axis(plane, cols_n // 2, lambda p: (row, p * 2 + core))
    axis_z = Axis(z_at, rows_n // 2, lambda p: (p * 2 + x_at, col))
    axes = (axis_core, axis_x, axis_y, axis_z)
    planes = cols_n // 2
    axis_chips = Axis(
        row * planes + plane,
        rows_n * planes,
        lambda p: (lax.div(p, planes), lax.rem(p, planes) * 2 + core),
    )

    has_up, has_down = row > 0, row < rows_n - 1
    has_left, has_right = col > 0, col < cols_n - 1
    near = {
        "up": (has_up, (row - 1, col)),
        "down": (has_down, (row + 1, col)),
        "left": (has_left, (row, col - 1)),
        "right": (has_right, (row, col + 1)),
        "up_left": (jnp.logical_and(has_up, has_left), (row - 1, col - 1)),
        "down_right": (jnp.logical_and(has_down, has_right), (row + 1, col + 1)),
    }
    links = Links(send_sem, recv_sem)

    loads = [
        pltpu.make_async_copy(source, target, load_sem.at[place])
        for place, (source, target) in enumerate(
            zip(
                early_hbm + late_hbm + kept_hbm + [offsets_hbm],
                early + late + kept + [offsets_ref],
            )
        )
    ]
    loads_early, loads_late, load_offsets = loads[:6], loads[6:-1], loads[-1]
    load_offsets.start()
    for place in (1, 2, 3, 4, 5, 0):
        loads_early[place].start()
    barrier = pltpu.get_barrier_semaphore()
    expected = sum(axis.size - 1 for axis in axes)
    for axis in axes:
        for step in range(1, axis.size):
            pl.semaphore_signal(
                barrier, inc=1, device_id=axis.device(axis.peer(step)), device_id_type=MESH
            )
    for there, device in near.values():
        expected = expected + there.astype(jnp.int32)

        @pl.when(there)
        def _():
            pl.semaphore_signal(barrier, inc=1, device_id=device, device_id_type=MESH)

    for load in loads_late:
        load.start()

    lane = lax.broadcasted_iota(jnp.int32, (CH, LANES), 1)
    lane_8 = lax.broadcasted_iota(jnp.int32, (SUBLANES, LANES), 1)
    load_offsets.wait()
    off_y = offsets_ref[0, 0, 0].astype(F32) / SUB
    off_x = offsets_ref[0, 0, 1].astype(F32) / SUB

    def fine_row(r):
        return fine[pl.ds(r, CH, stride=SR), :]

    def roll(value, shift):
        return pltpu.roll(value, shift % LANES, 1)

    coarse_s[...] = jnp.zeros(coarse_s.shape, F32)
    up_buf[...] = jnp.zeros(up_buf.shape, F32)
    loads_early[1].wait()
    loads_early[2].wait()
    for r in range(CR):
        coarse_s[r, :, :CC] = coarse[pl.ds(r, CH, stride=CR), :]
    up_buf[0] = fine_row(0)
    up_buf[1] = coarse_s[0]
    packed = jnp.zeros((CH, LANES), F32)
    for r in range(SR):
        packed = jnp.where(lane == r, roll(fine_row(r), r), packed)
    for r in range(CR):
        packed = jnp.where(lane == SR + r, roll(coarse_s[r], SR + r), packed)
    cp_buf[...] = packed

    pl.semaphore_wait(barrier, expected)

    def halo(source, target, towards, back):
        slot = links.take(1)
        copy = links.copy(source, target, near[towards][1], slot)
        arriving = links.copy(source, target, near[back][1], slot)

        @pl.when(near[towards][0])
        def _():
            copy.start()

        def finish():
            @pl.when(near[towards][0])
            def _():
                copy.wait_send()

            @pl.when(near[back][0])
            def _():
                arriving.wait_recv()

        return finish

    waits = [
        halo(up_buf, below_buf, "up", "down"),
        halo(cp_buf, right_cp, "left", "right"),
        halo(cp_buf, diag_cp, "up_left", "down_right"),
    ]
    for target, back in ((below_buf, "down"), (right_cp, "right"), (diag_cp, "down_right")):

        @pl.when(jnp.logical_not(near[back][0]))
        def _():
            target[...] = jnp.zeros(target.shape, F32)

    loads_early[3].wait()
    loads_early[4].wait()
    loads_early[5].wait()
    b_in_t[...] = w_in[...].astype(BF16)
    b_in[...] = w_in[...].T.astype(BF16)
    b_mid[...] = w_mid[...].astype(BF16)
    b_mid_t[...] = w_mid[...].T.astype(BF16)
    padded_out = jnp.concatenate([w_out[...], jnp.zeros((SUBLANES - OUT, HID), F32)], axis=0)
    b_out[...] = padded_out.astype(BF16)
    b_out_t[...] = padded_out.T.astype(BF16)
    cot_s[...] = jnp.zeros(cot_s.shape, BF16)
    vertex = lax.broadcasted_iota(jnp.int32, (LANES, LANES), 0)
    sample = lax.broadcasted_iota(jnp.int32, (LANES, LANES), 1)
    base = lax.div(sample, RATIO)
    fraction = (lax.rem(sample, RATIO).astype(F32) + off_x) / RATIO
    table = jnp.where(vertex == base, 1.0 - fraction, 0.0) + jnp.where(
        vertex == base + 1, fraction, 0.0
    )
    for wait in waits:
        wait()

    for r in range(SR + 1):
        value = fine_row(r) if r < SR else below_buf[0]
        edge = roll(right_cp[...], LANES - 1 - r) if r < SR else roll(diag_cp[...], LANES - 1)
        shifted = jnp.where(lane == LANES - 1, edge, roll(value, LANES - 1))
        across[r] = (1.0 - off_x) * value + off_x * shifted
    for r in range(CR + 1):
        value = coarse_s[r] if r < CR else below_buf[1]
        edge = roll(right_cp[...], CC - SR - r) if r < CR else roll(diag_cp[...], CC - SR)
        coarse_s[r] = jnp.where(lane == CC, edge, value)
    across_c[...] = dot(
        coarse_s[...].reshape((CR + 1) * CH, LANES), table, precision=lax.Precision.HIGHEST
    ).reshape(CR + 1, CH, LANES)

    def chunk_span(c):
        return pl.ds(pl.multiple_of(c * CHUNK, CHUNK), CHUNK)

    def spread_word(place, axis):
        for step in range(1, axis.size):
            pl.semaphore_signal(
                know_sem.at[place],
                inc=1,
                device_id=axis.device(axis.peer(step)),
                device_id_type=MESH,
            )

    def hear_word(place, axis):
        pl.semaphore_wait(know_sem.at[place], axis.size - 1)

    def forward(c):
        for k in range(GROUP):
            i = c * GROUP + k
            j = c * (GROUP // RATIO) + k // RATIO
            span = pl.ds(pl.multiple_of(i * SC, SC), SC)
            part = (k % RATIO + off_y) / RATIO
            feats[:CH, span] = ((1.0 - off_y) * across[i] + off_y * across[i + 1]).astype(BF16)
            feats[CH:, span] = ((1.0 - part) * across_c[j] + part * across_c[j + 1]).astype(BF16)
        span = chunk_span(c)
        act, slope = gate(dot(b_in[...], feats[:, span]))
        act_0[:, span] = act.astype(BF16)
        slope_0[:, span] = slope
        act, slope = gate(dot(b_mid[...], act_0[:, span]))
        act_1[:, span] = act.astype(BF16)
        slope_1[:, span] = slope
        colours = dot(b_out[...], act_1[:, span])
        for k in range(GROUP):
            pred[c * GROUP + k + 1] = colours[:, k * SC : (k + 1) * SC]

    order = [0, CHUNKS - 1] + list(range(1, CHUNKS - 1))

    def target_row(kind, r):
        found = targets[pl.ds(kind * OUT * SR + r, OUT, stride=SR), :]
        return jnp.concatenate([found, jnp.zeros((SUBLANES - OUT, LANES), F32)], axis=0)

    def send_columns(batch, groups):
        first_col = last_col = last_aim = jnp.zeros((SUBLANES, LANES), F32)
        for c in groups:
            for r in range(c * GROUP, (c + 1) * GROUP):
                first_col = jnp.where(lane_8 == r, roll(pred[r + 1], r), first_col)
                last_col = jnp.where(lane_8 == r, roll(pred[r + 1], r + 1), last_col)
                last_aim = jnp.where(lane_8 == r, roll(target_row(2, r), r + 1), last_aim)
        col_send[batch, 0] = first_col
        col_send[batch, 1] = last_col
        col_send[batch, 2] = last_aim
        return [
            halo(col_send.at[batch, 0], col_recv.at[batch, 0], "left", "right"),
            halo(col_send.at[batch, pl.ds(1, 2)], col_recv.at[batch, pl.ds(1, 2)], "right", "left"),
        ]

    spread_word(0, axis_x)
    for place in range(CHUNKS - 1):
        forward(order[place])
        if place == 0:
            hear_word(0, axis_x)
            spread_word(1, axis_y)
    hear_word(1, axis_y)
    loads_early[0].wait()
    edge_send[0, 0] = pred[1]
    edge_send[1, 0] = pred[SR]
    edge_send[1, 1] = target_row(1, SR - 1)
    early_waits = [
        halo(edge_send.at[0, 0], edge_recv.at[0, 0], "up", "down"),
        halo(edge_send.at[1], edge_recv.at[1], "down", "up"),
    ]
    early_waits += send_columns(0, order[:-1])
    for place, back in enumerate(("down", "up")):

        @pl.when(jnp.logical_not(near[back][0]))
        def _():
            edge_recv[place] = jnp.zeros(edge_recv.shape[1:], F32)

    forward(order[-1])
    last_waits = send_columns(1, order[-1:])
    for place, back in ((0, "right"), (1, "left"), (2, "left")):

        @pl.when(jnp.logical_not(near[back][0]))
        def _():
            for batch in range(2):
                col_recv[batch, place] = jnp.zeros(col_recv.shape[2:], F32)

    for wait in early_waits:
        wait()
    pred[SR + 1] = edge_recv[0, 0]
    above_error = jnp.where(has_up, (pred[1] - edge_recv[1, 0]) - edge_recv[1, 1], 0.0)

    def row_error(r):
        if r < 0:
            return above_error
        error = (pred[r + 2] - pred[r + 1]) - target_row(1, r)
        return jnp.where(has_down, error, 0.0) if r == SR - 1 else error

    def cotangent(c, batch):
        prior = row_error(c * GROUP - 1)
        for r in range(c * GROUP, (c + 1) * GROUP):
            here = pred[r + 1]
            error = row_error(r)
            edge = roll(col_recv[batch, 0], LANES - 1 - r)
            beside = jnp.where(lane_8 == LANES - 1, edge, roll(here, -1))
            col_error = (beside - here) - target_row(2, r)
            closed = jnp.logical_and(lane_8 == LANES - 1, jnp.logical_not(has_right))
            col_error = jnp.where(closed, 0.0, col_error)
            before = (here - roll(col_recv[batch, 1], -r)) - roll(col_recv[batch, 2], -r)
            before = jnp.where(has_left, before, 0.0)
            col_prior = jnp.where(lane_8 == 0, before, roll(col_error, 1))
            value_error = here - target_row(0, r)
            cot = (
                2.0 * LOSS_VALUE * value_error
                + 2.0 * (prior - error)
                + 2.0 * (col_prior - col_error)
            )
            kept = lax.broadcasted_iota(jnp.int32, (SUBLANES, LANES), 0) < OUT
            cot_s[:, r * SC : (r + 1) * SC] = jnp.where(kept, cot, 0.0).astype(BF16)
            prior = error

    def upper(c):
        span = chunk_span(c)
        delta_1[:, span] = (dot(b_out_t[...], cot_s[:, span]) * slope_1[:, span]).astype(BF16)

    for c in order[:-1]:
        cotangent(c, 0)
    for c in order[:-1]:
        upper(c)
    for wait in last_waits:
        wait()
    cotangent(order[-1], 1)
    upper(order[-1])
    grad_out[...] = dot_t(cot_s[...], act_1[...])
    outs = Total(links, grad_out, out_lands, axes)
    outs.start()

    half = HID // 2
    mid_rows = HID * half // LANES
    parts = 4
    part_rows = mid_rows // parts
    orders = ((axis_x, axis_y, axis_z), (axis_y, axis_x, axis_z))
    mids = [
        Scatter(links, mid_own, k * part_rows, part_rows, orders[k % 2], lands[k * 3 : k * 3 + 3])
        for k in range(parts)
    ]

    def mid_half(which, target):
        upper = delta_1[pl.ds(pl.multiple_of(which * half, half), half), :]
        block = dot_t(upper, act_0[...])
        for part in range(HID // LANES):
            target[part * half : (part + 1) * half, :] = block[:, part * LANES : (part + 1) * LANES]

    partner = axis_core.device(1 - core)
    part_span = lambda k: pl.ds(k * part_rows, part_rows)
    pairs = [
        links.copy(
            mid_away.at[part_span(k)], mid_pair.at[part_span(k)], partner, links.take(1)
        )
        for k in range(parts)
    ]
    mid_half(1 - core, mid_away)
    for pair in pairs:
        pair.start()
    mid_half(core, mid_own)
    for k in range(parts):
        pairs[k].wait()
        mid_own[part_span(k)] += mid_pair[part_span(k)]
        mids[k].start(0)

    grad_in[...] = jnp.zeros(grad_in.shape, F32)

    def lower(c):
        span = chunk_span(c)
        delta = (dot(b_mid_t[...], delta_1[:, span]) * slope_0[:, span]).astype(BF16)
        grad_in[...] += dot_t(feats[:, span], delta)
        spread = dot(b_in_t[...], delta)
        for k in range(GROUP):
            fgrad[c * GROUP + k] = spread[:, k * SC : (k + 1) * SC]

    def advance(which, stage):
        for k in which:
            mids[k].finish(stage)
            if stage < 2:
                mids[k].start(stage + 1)

    half_chunks = CHUNKS // 2
    for c in range(half_chunks):
        lower(c)
    outs.finish()
    advance((0, 1), 0)
    for c in range(half_chunks, CHUNKS - 1):
        lower(c)
    outs.finish()
    advance((2, 3), 0)
    lower(CHUNKS - 1)

    blocks = HID // LANES
    inputs = 2 * CH
    in_rows = inputs * blocks // 2
    own_rows = in_own.shape[0] // axis_chips.size

    def in_half(which, target):
        for choice in range(2):

            @pl.when(which == choice)
            def _():
                for part in range(blocks // 2):
                    at = (choice * (blocks // 2) + part) * LANES
                    target[part * inputs : (part + 1) * inputs, :] = grad_in[:, at : at + LANES]
        if target.shape[0] > in_rows:
            target[in_rows:, :] = jnp.zeros((target.shape[0] - in_rows, LANES), F32)

    in_half(1 - core, in_away)
    pair_in = links.copy(in_away, in_pair, partner, links.take(1))
    pair_in.start()
    in_half(core, in_own)

    def own_span(place):
        return pl.ds(aligned(place * own_rows), own_rows)

    in_crowd = Crowd(
        links, axis_chips, lambda peer: in_own.at[own_span(peer)], lambda me: in_land.at[me]
    )
    advance((0, 1), 1)

    last = SR
    bottom = None
    packed = jnp.zeros((CH, LANES), F32)
    zero = jnp.zeros((CH, LANES), F32)
    for r in range(SR + 1):
        value = zero
        if r < SR:
            value = (1.0 - off_y) * fgrad[r, :CH]
        if r > 0:
            value = value + off_y * fgrad[r - 1, :CH]
        moved = off_x * roll(value, 1)
        out = (1.0 - off_x) * value + jnp.where(lane == 0, 0.0, moved)
        at = r if r < SR else SR + CR
        packed = jnp.where(lane == at, roll(moved, at), packed)
        if r < SR:
            fine_g[r] = out
        else:
            down_buf[0] = out
    for j in range(CR + 1):
        value = zero
        for k in range(RATIO):
            part = (k + off_y) / RATIO
            if j < CR:
                value = value + (1.0 - part) * fgrad[j * RATIO + k, CH:]
            if j > 0:
                value = value + part * fgrad[(j - 1) * RATIO + k, CH:]
        coarse_s[j] = value
    spread = dot_t(
        coarse_s[...].reshape((CR + 1) * CH, LANES), table, precision=lax.Precision.HIGHEST
    ).reshape(CR + 1, CH, LANES)
    for j in range(CR + 1):
        value = spread[j]
        at = SR + j if j < CR else SR + CR + 1
        packed = jnp.where(lane == at, roll(value, at - CC), packed)
        value = jnp.where(lane < CC, value, 0.0)
        if j < CR:
            coarse_g[j] = value
        else:
            down_buf[1] = value
    q_buf[...] = packed
    waits = [
        halo(down_buf, above_buf, "down", "up"),
        halo(q_buf, left_q, "right", "left"),
        halo(q_buf, diag_q, "down_right", "up_left"),
    ]
    for target, back in ((above_buf, "up"), (left_q, "left"), (diag_q, "up_left")):

        @pl.when(jnp.logical_not(near[back][0]))
        def _():
            target[...] = jnp.zeros(target.shape, F32)

    outs.finish()
    pair_in.wait()
    in_own[...] += in_pair[...]
    in_crowd.start()
    advance((2, 3), 1)
    for wait in waits:
        wait()
    fine_g[0] += above_buf[0] + jnp.where(lane == 0, roll(diag_q[...], -(SR + CR)), 0.0)
    coarse_g[0] += above_buf[1] + jnp.where(lane == 0, roll(diag_q[...], -(SR + CR + 1)), 0.0)
    squares = jnp.zeros((CH, LANES), F32)
    for r in range(SR):
        value = fine_g[r] + jnp.where(lane == 0, roll(left_q[...], -r), 0.0)
        fine_g[r] = value
        squares += value * value
    for j in range(CR):
        value = coarse_g[j] + jnp.where(lane == 0, roll(left_q[...], -(SR + j)), 0.0)
        coarse_g[j] = value
        squares += value * value
    total = squares[:SUBLANES]
    for part in range(1, CH // SUBLANES):
        total = total + squares[part * SUBLANES : (part + 1) * SUBLANES]
    total_mine[...] = total
    totals = Total(links, total_mine, total_lands, (axis_core, axis_chips))
    totals.start()
    gathers = [Gather(scatter, mid_full.at[core]) for scatter in mids]

    def settle(which):
        for k in which:
            mids[k].finish(2)
            gathers[k].place()
            gathers[k].start(2)

    def regain(which, stage):
        for k in which:
            gathers[k].finish(stage)
            if stage > 0:
                gathers[k].start(stage - 1)

    settle((0, 1))
    mine = own_span(axis_chips.me)
    in_land[axis_chips.me] = in_own[mine]
    count = axis_chips.size - 1
    in_crowd.wait(in_own.at[pl.ds(0, count * own_rows)], in_land.at[pl.ds(0, count)])
    found = in_land[0]
    for place in range(1, axis_chips.size):
        found = found + in_land[place]
    in_full[core, mine] = found
    in_block = in_full.at[core, mine]
    in_back = Crowd(links, axis_chips, lambda peer: in_block, lambda me: in_block)
    in_back.start()
    settle((2, 3))
    totals.finish()
    out_full[...] = outs.finish()
    regain((0, 1), 2)
    regain((2, 3), 2)
    grid_total = totals.finish()

    for load in loads_late:
        load.wait()
    fine_first, fine_second, coarse_first, coarse_second = late
    entries = CH * (SR * SC + CR * CC) * rows_n * cols_n
    grid_scale = clip_factor(jnp.sum(grid_total, keepdims=True), entries)
    for r in range(SR):
        span = pl.ds(r, CH, stride=SR)
        fine_out[span, :] = adam_step(fine_g[r], fine_first[span, :], fine_second[span, :], grid_scale)
    for j in range(CR):
        span = pl.ds(j, CH, stride=CR)
        coarse_out[span, :] = adam_step(
            coarse_g[j, :, :CC], coarse_first[span, :], coarse_second[span, :], grid_scale
        )
    in_span = in_full.at[core, pl.ds(0, count * own_rows)]
    in_back.wait(in_span, in_span)
    last_in = links.copy(in_full.at[core], in_full.at[core], partner, links.take(1))
    last_in.start()
    regain((0, 1), 1)
    regain((2, 3), 1)

    def across_pair(k):
        block = mid_full.at[core, part_span(k)]
        copy = links.copy(block, block, partner, links.take(1))
        copy.start()
        return copy

    lasts = []
    for k in range(parts):
        gathers[k].finish(0)
        lasts.append(across_pair(k))
    last_in.wait()
    for copy in lasts:
        copy.wait()
    assert links.used <= dims["COPIES"]


def adam_kernel(
    fine_step,
    coarse_step,
    mid_full,
    in_full,
    out_full,
    in_first,
    in_second,
    mid_first,
    mid_second,
    out_first,
    out_second,
    fine_out,
    coarse_out,
    in_out,
    mid_out,
    out_out,
    in_step,
    mid_step,
    out_step,
    sems,
):
    writes = []

    def write(source, target):
        copy = pltpu.make_async_copy(source, target, sems.at[len(writes)])
        copy.start()
        writes.append(copy)

    write(fine_step, fine_out)
    write(coarse_step, coarse_out)
    inputs, hidden = in_step.shape
    outputs = out_step.shape[0]
    half, blocks = hidden // 2, hidden // LANES
    parts = [mid_full[which, :, :] for which in range(2)]
    parts += [in_full[which, : inputs * blocks // 2, :] for which in range(2)]
    parts += [out_full[:, part * LANES : (part + 1) * LANES] for part in range(blocks)]
    squares = jnp.zeros((SUBLANES, LANES), F32)
    for value in parts:
        value = (value * value).reshape(-1, SUBLANES, LANES)
        squares += jnp.sum(value, axis=0)
    scale = clip_factor(jnp.sum(squares, keepdims=True), hidden * (hidden + inputs + outputs))
    for which in range(2):
        span = slice(which * half, (which + 1) * half)
        for part in range(blocks):
            lanes = slice(part * LANES, (part + 1) * LANES)
            mid_step[span, lanes] = adam_step(
                mid_full[which, part * half : (part + 1) * half, :],
                mid_first[span, lanes],
                mid_second[span, lanes],
                scale,
            )
        write(mid_step.at[pl.ds(which * half, half)], mid_out.at[pl.ds(which * half, half)])
    out_step[...] = adam_step(out_full[:outputs, :], out_first[...], out_second[...], scale)
    write(out_step, out_out)
    for which in range(2):
        for part in range(blocks // 2):
            at = (which * (blocks // 2) + part) * LANES
            lanes = slice(at, at + LANES)
            in_step[:, lanes] = adam_step(
                in_full[which, part * inputs : (part + 1) * inputs, :],
                in_first[:, lanes],
                in_second[:, lanes],
                scale,
            )
    write(in_step, in_out)
    for copy in writes:
        copy.wait()


def shards(
    offsets,
    targets,
    grid_fine,
    grid_coarse,
    weight_in,
    weight_mid,
    weight_out,
    fine_first,
    fine_second,
    coarse_first,
    coarse_second,
    in_first,
    in_second,
    mid_first,
    mid_second,
    out_first,
    out_second,
):
    CH, SR, SC = grid_fine.shape
    CR, CC = grid_coarse.shape[1:]
    HID = weight_in.shape[0]
    OUT = weight_out.shape[0]
    S = SR * SC
    rows_n, cols_n = lax.axis_size("row"), lax.axis_size("col")
    sizes_x, sizes_y, sizes_z = 2, cols_n // 2, rows_n // 2
    peers = (sizes_x - 1) + (sizes_y - 1) + (sizes_z - 1)
    parts = 4
    copies = 2 * parts * (peers + 1) + 24
    chips = sizes_x * sizes_y * sizes_z
    in_rows = CH * HID // LANES
    in_rows = -(-in_rows // (chips * SUBLANES)) * chips * SUBLANES
    mid_rows = HID * HID // 2 // LANES
    dims = dict(CH=CH, SR=SR, SC=SC, CR=CR, CC=CC, HID=HID, OUT=OUT, COPIES=copies, GROUP=8)

    flat = lambda grid: grid.reshape(-1, grid.shape[-1])
    early = (
        flat(targets),
        flat(grid_fine),
        flat(grid_coarse),
        weight_in.T,
        weight_mid[0],
        weight_out,
    )
    late = (flat(fine_first), flat(fine_second), flat(coarse_first), flat(coarse_second))
    vmem = lambda *shape: pltpu.VMEM(shape, F32)
    low = lambda *shape: pltpu.VMEM(shape, BF16)

    def landing(rows, sizes):
        found = []
        for size in sizes:
            rows = rows // size
            found.append(vmem(max(size - 1, 1), rows, LANES))
        return found

    orders = ((sizes_x, sizes_y, sizes_z), (sizes_y, sizes_x, sizes_z))
    kept = (in_first.T, in_second.T, mid_first[0], mid_second[0], out_first, out_second)
    scratch = [pltpu.SMEM(offsets.shape, jnp.int32)]
    scratch += [pltpu.VMEM(a.shape, F32) for a in early + late]
    scratch += [
        vmem(2, CH, LANES),
        vmem(CH, LANES),
        vmem(2, CH, LANES),
        vmem(CH, LANES),
        vmem(CH, LANES),
        vmem(CR + 1, CH, LANES),
        vmem(SR + 1, CH, LANES),
        vmem(CR + 1, CH, LANES),
        low(HID, 2 * CH),
        low(2 * CH, HID),
        low(HID, HID),
        low(HID, HID),
        low(SUBLANES, HID),
        low(HID, SUBLANES),
        low(2 * CH, S),
        low(HID, S),
        low(HID, S),
        vmem(HID, S),
        vmem(HID, S),
        low(HID, S),
        vmem(SR + 2, SUBLANES, LANES),
        vmem(2, 2, SUBLANES, LANES),
        vmem(2, 2, SUBLANES, LANES),
        vmem(2, 3, SUBLANES, LANES),
        vmem(2, 3, SUBLANES, LANES),
        low(SUBLANES, S),
        vmem(SR, 2 * CH, LANES),
        vmem(2, CH, LANES),
        vmem(CH, LANES),
        vmem(2, CH, LANES),
        vmem(CH, LANES),
        vmem(CH, LANES),
        vmem(SR, CH, LANES),
        vmem(CR, CH, LANES),
        vmem(2 * CH, HID),
        vmem(SUBLANES, HID),
        vmem(mid_rows, LANES),
        vmem(mid_rows, LANES),
        vmem(mid_rows, LANES),
        vmem(in_rows, LANES),
        vmem(in_rows, LANES),
        vmem(in_rows, LANES),
        vmem(chips, in_rows // chips, LANES),
        vmem(SUBLANES, LANES),
    ]
    scratch += [vmem(size, SUBLANES, HID) for size in (2, sizes_x, sizes_y, sizes_z)]
    scratch += [vmem(size, SUBLANES, LANES) for size in (2, chips)]
    for part in range(parts):
        scratch += landing(mid_rows // parts, orders[part % 2])
    scratch += [
        pltpu.SemaphoreType.DMA((len(early) + len(late) + len(kept) + 1,)),
        pltpu.SemaphoreType.DMA((copies,)),
        pltpu.SemaphoreType.DMA((copies,)),
        pltpu.SemaphoreType.REGULAR((2,)),
    ]
    outs = (
        (CH * SR, SC),
        (CH * CR, CC),
        (2, mid_rows, LANES),
        (2, in_rows, LANES),
        (SUBLANES, HID),
    ) + tuple(a.shape for a in kept)
    far = pl.BlockSpec(memory_space=pltpu.HBM)
    whole = pl.BlockSpec(memory_space=pltpu.VMEM)
    found = pl.pallas_call(
        functools.partial(step_kernel, dims),
        out_shape=[jax.ShapeDtypeStruct(shape, F32) for shape in outs],
        in_specs=[far] * (1 + len(early) + len(late) + len(kept)),
        out_specs=[whole] * len(outs),
        scratch_shapes=scratch,
        compiler_params=pltpu.CompilerParams(
            collective_id=0, has_side_effects=True, vmem_limit_bytes=48 * 1024 * 1024
        ),
        name="field",
    )(*[pltpu.with_memory_space_constraint(a, pltpu.HBM) for a in (offsets, *early, *late, *kept)])
    steps = ((CH * SR, SC), (CH * CR, CC), (2 * CH, HID), (HID, HID), (OUT, HID))
    fine_step, coarse_step, in_step, mid_step, out_step = pl.pallas_call(
        adam_kernel,
        out_shape=[jax.ShapeDtypeStruct(shape, F32) for shape in steps],
        in_specs=[whole] * len(found),
        out_specs=[far] * len(steps),
        scratch_shapes=[pltpu.VMEM(shape, F32) for shape in steps[2:]]
        + [pltpu.SemaphoreType.DMA((4 + 2 * HID // LANES,))],
        compiler_params=pltpu.CompilerParams(vmem_limit_bytes=8 * 1024 * 1024),
        name="adam",
    )(*found)
    return (
        fine_step.reshape(grid_fine.shape),
        coarse_step.reshape(grid_coarse.shape),
        in_step.T,
        mid_step[None],
        out_step,
    )


def solution(mesh):
    tile, copied = P(None, "row", "col"), P()
    placed = (P("row", "col", None), P(None, None, "row", "col"), tile, tile)
    placed += (copied,) * 3 + (tile,) * 4 + (copied,) * 6
    return jax.shard_map(
        shards,
        mesh=mesh,
        in_specs=placed,
        out_specs=(tile, tile, copied, copied, copied),
        check_vma=False,
    )
```

time: 70.8 us -> 57 us (0.81)
  Pallas kernels: 64.2 us -> 56 us
  local copies, waits for them, and re-layouts: 5.79 us -> 0 us
    pallas_call x1, Pallas kernels: 64.2 us -> 54.1 us  [shards(): pl.pallas_call(functools.partial(step_kernel, dims), out_shape=[jax.Shape...]
    unnamed x11 -> x0, local copies, waits for them, and re-layouts: 5.79 us -> none
    pallas_call x0 -> x1, Pallas kernels: none -> 1.97 us  [shards(): pl.pallas_call(adam_kernel, out_shape=[jax.ShapeDtypeStruct(shape, F32) f...]
where the time goes in v2:
time: 57 us; the launch traced here: 56.8 us
  Pallas kernels  56 us (98%)
  between operations  0.81 us (1%)
    pallas_call x1, Pallas kernels, shards(): pl.pallas_call(functools.partial(step_kernel, dims), out_shape=[jax.Shape...  54.1 us
    pallas_call x1, Pallas kernels, shards(): pl.pallas_call(adam_kernel, out_shape=[jax.ShapeDtypeStruct(shape, F32) f...  1.97 us

profile of v2, /device:TPU:0, one launch (start us, length us, event | category | flops | bytes accessed | tf_op | source)
XLA Modules:
  0.0 56.8 jit_solution(2763335607402641817)
XLA Ops:
  0.6 54.1 %field.1 = (f32[1024,128]{1,0:T(8,128)S(1)}, f32[256,32]{1,0:T(8,128)S(1)}, f32[2,1024,128]{2,1,0:T(8,128)S(1)}, f32[2,128,128]{2,1,0:T(8,128)S(1)}, f32[8,512]{...) custom-call(s32[1,1,2]{2,1,0:T(1,128)} %refs_0_.1, ...), custom_call_target="tpu_custom_call" | custom-call | tf_op jit(solution)/shard_map/field/pallas_call | solution.py:990
  54.7 2.0 %adam.1 = (f32[1024,128]{1,0:T(8,128)}, f32[256,32]{1,0:T(8,128)}, f32[64,512]{1,0:T(8,128)}, f32[512,512]{1,0:T(8,128)}, f32[3,512]{1,0:T(4,128)}) custom-call(f32[1024,128]{1,0:T(8,128)S(1)} %get-tuple-element.21.fine_step, f32[256,32]{1,0:T(8,128)S(1)} %get-tuple-element.22.coarse_step, f32[2,1024,128]{2,1,0:T(8,128)S(1)} %get-tuple-element.23.mid_full, ...), custom_call_target="tpu_custom_call" | custom-call | tf_op jit(solution)/shard_map/adam/pallas_call | solution.py:1002

commit v3 on v2

--- a/solution.py
+++ b/solution.py
@@ -49,10 +49,13 @@
     return dot(former, latter, ((1,), (1,)), precision)
 
 
-def gate(pre_act):
-    sigmoid = 0.5 * jnp.tanh(0.5 * pre_act) + 0.5
-    act = pre_act * sigmoid
-    return act, sigmoid + act * (1.0 - sigmoid)
+def silu_of_half(half):
+    return half + half * jnp.tanh(half)
+
+
+def slope_of_half(half):
+    bend = jnp.tanh(half)
+    return (1.0 + bend) * ((1.0 + half) - half * bend)
 
 
 class Axis:
@@ -233,8 +236,8 @@
         feats,
         act_0,
         act_1,
-        slope_0,
-        slope_1,
+        half_0,
+        half_1,
         delta_1,
         pred,
         edge_send,
@@ -258,12 +261,11 @@
         in_away,
         in_own,
         in_pair,
-        in_land,
         total_mine,
-    ) = take(44)
+    ) = take(43)
     out_lands = take(4)
     total_lands = take(2)
-    lands = take(12)
+    lands = take(14)
     load_sem, send_sem, recv_sem, know_sem = take(4)
 
     rows_n, cols_n = lax.axis_size("row"), lax.axis_size("col")
@@ -282,6 +284,11 @@
     axis_z = Axis(z_at, rows_n // 2, lambda p: (p * 2 + x_at, col))
     axes = (axis_core, axis_x, axis_y, axis_z)
     planes = cols_n // 2
+    axis_plane = Axis(
+        x_at * planes + plane,
+        2 * planes,
+        lambda p: (z_at * 2 + lax.div(p, planes), lax.rem(p, planes) * 2 + core),
+    )
     axis_chips = Axis(
         row * planes + plane,
         rows_n * planes,
@@ -394,12 +401,13 @@
     loads_early[4].wait()
     loads_early[5].wait()
     b_in_t[...] = w_in[...].astype(BF16)
-    b_in[...] = w_in[...].T.astype(BF16)
-    b_mid[...] = w_mid[...].astype(BF16)
-    b_mid_t[...] = w_mid[...].T.astype(BF16)
+    b_in[...] = (0.5 * w_in[...]).T.astype(BF16)
+    halved = 0.5 * w_mid[...]
+    b_mid[...] = halved.astype(BF16)
+    b_mid_t[...] = halved.T.astype(BF16)
     padded_out = jnp.concatenate([w_out[...], jnp.zeros((SUBLANES - OUT, HID), F32)], axis=0)
     b_out[...] = padded_out.astype(BF16)
-    b_out_t[...] = padded_out.T.astype(BF16)
+    b_out_t[...] = (0.5 * padded_out).T.astype(BF16)
     cot_s[...] = jnp.zeros(cot_s.shape, BF16)
     vertex = lax.broadcasted_iota(jnp.int32, (LANES, LANES), 0)
     sample = lax.broadcasted_iota(jnp.int32, (LANES, LANES), 1)
@@ -425,7 +433,7 @@
     ).reshape(CR + 1, CH, LANES)
 
     def chunk_span(c):
-        return pl.ds(pl.multiple_of(c * CHUNK, CHUNK), CHUNK)
+        return slice(c * CHUNK, (c + 1) * CHUNK)
 
     def spread_word(place, axis):
         for step in range(1, axis.size):
@@ -443,17 +451,15 @@
         for k in range(GROUP):
             i = c * GROUP + k
             j = c * (GROUP // RATIO) + k // RATIO
-            span = pl.ds(pl.multiple_of(i * SC, SC), SC)
+            span = slice(i * SC, (i + 1) * SC)
             part = (k % RATIO + off_y) / RATIO
             feats[:CH, span] = ((1.0 - off_y) * across[i] + off_y * across[i + 1]).astype(BF16)
             feats[CH:, span] = ((1.0 - part) * across_c[j] + part * across_c[j + 1]).astype(BF16)
         span = chunk_span(c)
-        act, slope = gate(dot(b_in[...], feats[:, span]))
-        act_0[:, span] = act.astype(BF16)
-        slope_0[:, span] = slope
-        act, slope = gate(dot(b_mid[...], act_0[:, span]))
-        act_1[:, span] = act.astype(BF16)
-        slope_1[:, span] = slope
+        half_0[:, span] = dot(b_in[...], feats[:, span])
+        act_0[:, span] = silu_of_half(half_0[:, span]).astype(BF16)
+        half_1[:, span] = dot(b_mid[...], act_0[:, span])
+        act_1[:, span] = silu_of_half(half_1[:, span]).astype(BF16)
         colours = dot(b_out[...], act_1[:, span])
         for k in range(GROUP):
             pred[c * GROUP + k + 1] = colours[:, k * SC : (k + 1) * SC]
@@ -546,7 +552,8 @@
 
     def upper(c):
         span = chunk_span(c)
-        delta_1[:, span] = (dot(b_out_t[...], cot_s[:, span]) * slope_1[:, span]).astype(BF16)
+        slope = slope_of_half(half_1[:, span])
+        delta_1[:, span] = (dot(b_out_t[...], cot_s[:, span]) * slope).astype(BF16)
 
     for c in order[:-1]:
         cotangent(c, 0)
@@ -556,9 +563,6 @@
         wait()
     cotangent(order[-1], 1)
     upper(order[-1])
-    grad_out[...] = dot_t(cot_s[...], act_1[...])
-    outs = Total(links, grad_out, out_lands, axes)
-    outs.start()
 
     half = HID // 2
     mid_rows = HID * half // LANES
@@ -569,6 +573,9 @@
         Scatter(links, mid_own, k * part_rows, part_rows, orders[k % 2], lands[k * 3 : k * 3 + 3])
         for k in range(parts)
     ]
+    mids.append(
+        Scatter(links, in_own, 0, in_own.shape[0], (axis_plane, axis_z), lands[3 * parts :])
+    )
 
     def mid_half(which, target):
         upper = delta_1[pl.ds(pl.multiple_of(which * half, half), half), :]
@@ -593,11 +600,15 @@
         mid_own[part_span(k)] += mid_pair[part_span(k)]
         mids[k].start(0)
 
+    grad_out[...] = dot_t(cot_s[...], act_1[...])[:OUT]
+    outs = Total(links, grad_out, out_lands, axes)
+    outs.start()
     grad_in[...] = jnp.zeros(grad_in.shape, F32)
 
     def lower(c):
         span = chunk_span(c)
-        delta = (dot(b_mid_t[...], delta_1[:, span]) * slope_0[:, span]).astype(BF16)
+        slope = slope_of_half(half_0[:, span])
+        delta = (dot(b_mid_t[...], delta_1[:, span]) * slope).astype(BF16)
         grad_in[...] += dot_t(feats[:, span], delta)
         spread = dot(b_in_t[...], delta)
         for k in range(GROUP):
@@ -606,7 +617,7 @@
     def advance(which, stage):
         for k in which:
             mids[k].finish(stage)
-            if stage < 2:
+            if stage + 1 < len(mids[k].axes):
                 mids[k].start(stage + 1)
 
     half_chunks = CHUNKS // 2
@@ -623,7 +634,6 @@
     blocks = HID // LANES
     inputs = 2 * CH
     in_rows = inputs * blocks // 2
-    own_rows = in_own.shape[0] // axis_chips.size
 
     def in_half(which, target):
         for choice in range(2):
@@ -641,12 +651,6 @@
     pair_in.start()
     in_half(core, in_own)
 
-    def own_span(place):
-        return pl.ds(aligned(place * own_rows), own_rows)
-
-    in_crowd = Crowd(
-        links, axis_chips, lambda peer: in_own.at[own_span(peer)], lambda me: in_land.at[me]
-    )
     advance((0, 1), 1)
 
     last = SR
@@ -700,11 +704,28 @@
         def _():
             target[...] = jnp.zeros(target.shape, F32)
 
+    advance((2, 3), 1)
     outs.finish()
     pair_in.wait()
     in_own[...] += in_pair[...]
-    in_crowd.start()
-    advance((2, 3), 1)
+    mids[parts].start(0)
+    gathers = [Gather(scatter, mid_full.at[core]) for scatter in mids[:parts]]
+    gathers.append(Gather(mids[parts], in_full.at[core]))
+
+    def settle(which):
+        for k in which:
+            last_stage = len(mids[k].axes) - 1
+            mids[k].finish(last_stage)
+            gathers[k].place()
+            gathers[k].start(last_stage)
+
+    def regain(which, stage):
+        for k in which:
+            gathers[k].finish(stage)
+            if stage > 0:
+                gathers[k].start(stage - 1)
+
+    settle((0, 1))
     for wait in waits:
         wait()
     fine_g[0] += above_buf[0] + jnp.where(lane == 0, roll(diag_q[...], -(SR + CR)), 0.0)
@@ -721,40 +742,19 @@
     total = squares[:SUBLANES]
     for part in range(1, CH // SUBLANES):
         total = total + squares[part * SUBLANES : (part + 1) * SUBLANES]
-    total_mine[...] = total
+    total_mine[...] = jnp.sum(total, axis=0, keepdims=True)
     totals = Total(links, total_mine, total_lands, (axis_core, axis_chips))
     totals.start()
-    gathers = [Gather(scatter, mid_full.at[core]) for scatter in mids]
-
-    def settle(which):
-        for k in which:
-            mids[k].finish(2)
-            gathers[k].place()
-            gathers[k].start(2)
-
-    def regain(which, stage):
-        for k in which:
-            gathers[k].finish(stage)
-            if stage > 0:
-                gathers[k].start(stage - 1)
-
-    settle((0, 1))
-    mine = own_span(axis_chips.me)
-    in_land[axis_chips.me] = in_own[mine]
-    count = axis_chips.size - 1
-    in_crowd.wait(in_own.at[pl.ds(0, count * own_rows)], in_land.at[pl.ds(0, count)])
-    found = in_land[0]
-    for place in range(1, axis_chips.size):
-        found = found + in_land[place]
-    in_full[core, mine] = found
-    in_block = in_full.at[core, mine]
-    in_back = Crowd(links, axis_chips, lambda peer: in_block, lambda me: in_block)
-    in_back.start()
+    advance((parts,), 0)
     settle((2, 3))
     totals.finish()
+    regain((0, 1), 2)
+    settle((parts,))
     out_full[...] = outs.finish()
-    regain((0, 1), 2)
     regain((2, 3), 2)
+    regain((0, 1), 1)
+    regain((2, 3), 1)
+    regain((parts,), 1)
     grid_total = totals.finish()
 
     for load in loads_late:
@@ -770,13 +770,6 @@
         coarse_out[span, :] = adam_step(
             coarse_g[j, :, :CC], coarse_first[span, :], coarse_second[span, :], grid_scale
         )
-    in_span = in_full.at[core, pl.ds(0, count * own_rows)]
-    in_back.wait(in_span, in_span)
-    last_in = links.copy(in_full.at[core], in_full.at[core], partner, links.take(1))
-    last_in.start()
-    regain((0, 1), 1)
-    regain((2, 3), 1)
-
     def across_pair(k):
         block = mid_full.at[core, part_span(k)]
         copy = links.copy(block, block, partner, links.take(1))
@@ -787,7 +780,11 @@
     for k in range(parts):
         gathers[k].finish(0)
         lasts.append(across_pair(k))
-    last_in.wait()
+        if k == 1:
+            gathers[parts].finish(0)
+            last_in = links.copy(in_full.at[core], in_full.at[core], partner, links.take(1))
+            last_in.start()
+            lasts.append(last_in)
     for copy in lasts:
         copy.wait()
     assert links.used <= dims["COPIES"]
@@ -829,12 +826,12 @@
     half, blocks = hidden // 2, hidden // LANES
     parts = [mid_full[which, :, :] for which in range(2)]
     parts += [in_full[which, : inputs * blocks // 2, :] for which in range(2)]
-    parts += [out_full[:, part * LANES : (part + 1) * LANES] for part in range(blocks)]
     squares = jnp.zeros((SUBLANES, LANES), F32)
     for value in parts:
         value = (value * value).reshape(-1, SUBLANES, LANES)
         squares += jnp.sum(value, axis=0)
-    scale = clip_factor(jnp.sum(squares, keepdims=True), hidden * (hidden + inputs + outputs))
+    total = jnp.sum(squares, keepdims=True) + jnp.sum(out_full[...] * out_full[...], keepdims=True)
+    scale = clip_factor(total, hidden * (hidden + inputs + outputs))
     for which in range(2):
         span = slice(which * half, (which + 1) * half)
         for part in range(blocks):
@@ -846,7 +843,7 @@
                 scale,
             )
         write(mid_step.at[pl.ds(which * half, half)], mid_out.at[pl.ds(which * half, half)])
-    out_step[...] = adam_step(out_full[:outputs, :], out_first[...], out_second[...], scale)
+    out_step[...] = adam_step(out_full[...], out_first[...], out_second[...], scale)
     write(out_step, out_out)
     for which in range(2):
         for part in range(blocks // 2):
@@ -891,7 +888,7 @@
     sizes_x, sizes_y, sizes_z = 2, cols_n // 2, rows_n // 2
     peers = (sizes_x - 1) + (sizes_y - 1) + (sizes_z - 1)
     parts = 4
-    copies = 2 * parts * (peers + 1) + 24
+    copies = 2 * parts * (peers + 1) + 2 * (sizes_x * sizes_y + sizes_z) + 24
     chips = sizes_x * sizes_y * sizes_z
     in_rows = CH * HID // LANES
     in_rows = -(-in_rows // (chips * SUBLANES)) * chips * SUBLANES
@@ -958,20 +955,20 @@
         vmem(SR, CH, LANES),
         vmem(CR, CH, LANES),
         vmem(2 * CH, HID),
-        vmem(SUBLANES, HID),
+        vmem(OUT, HID),
         vmem(mid_rows, LANES),
         vmem(mid_rows, LANES),
         vmem(mid_rows, LANES),
         vmem(in_rows, LANES),
         vmem(in_rows, LANES),
         vmem(in_rows, LANES),
-        vmem(chips, in_rows // chips, LANES),
-        vmem(SUBLANES, LANES),
+        vmem(1, LANES),
     ]
-    scratch += [vmem(size, SUBLANES, HID) for size in (2, sizes_x, sizes_y, sizes_z)]
-    scratch += [vmem(size, SUBLANES, LANES) for size in (2, chips)]
+    scratch += [vmem(size, OUT, HID) for size in (2, sizes_x, sizes_y, sizes_z)]
+    scratch += [vmem(size, 1, LANES) for size in (2, chips)]
     for part in range(parts):
         scratch += landing(mid_rows // parts, orders[part % 2])
+    scratch += landing(in_rows, (sizes_x * sizes_y, sizes_z))
     scratch += [
         pltpu.SemaphoreType.DMA((len(early) + len(late) + len(kept) + 1,)),
         pltpu.SemaphoreType.DMA((copies,)),
@@ -983,7 +980,7 @@
         (CH * CR, CC),
         (2, mid_rows, LANES),
         (2, in_rows, LANES),
-        (SUBLANES, HID),
+        (OUT, HID),
     ) + tuple(a.shape for a in kept)
     far = pl.BlockSpec(memory_space=pltpu.HBM)
     whole = pl.BlockSpec(memory_space=pltpu.VMEM)

time: 57 us -> 52.7 us (0.925)
  Pallas kernels: 56 us -> 51.7 us
    pallas_call x1, Pallas kernels: 54.1 us -> 49.7 us  [shards(): pl.pallas_call(functools.partial(step_kernel, dims), out_shape=[jax.Shape...]
where the time goes in v3:
time: 52.7 us; the launch traced here: 52.6 us
  Pallas kernels  51.7 us (98%)
  between operations  0.83 us (2%)
    pallas_call x1, Pallas kernels, shards(): pl.pallas_call(functools.partial(step_kernel, dims), out_shape=[jax.Shape...  49.7 us
    pallas_call x1, Pallas kernels, shards(): pl.pallas_call(adam_kernel, out_shape=[jax.ShapeDtypeStruct(shape, F32) f...  2.01 us

profile of v3, /device:TPU:0, one launch (start us, length us, event | category | flops | bytes accessed | tf_op | source)
XLA Modules:
  0.0 52.6 jit_solution(3729918485606844996)
XLA Ops:
  0.6 49.7 %field.1 = (f32[1024,128]{1,0:T(8,128)S(1)}, f32[256,32]{1,0:T(8,128)S(1)}, f32[2,1024,128]{2,1,0:T(8,128)S(1)}, f32[2,128,128]{2,1,0:T(8,128)S(1)}, f32[3,512]{...) custom-call(s32[1,1,2]{2,1,0:T(1,128)} %refs_0_.1, ...), custom_call_target="tpu_custom_call" | custom-call | tf_op jit(solution)/shard_map/field/pallas_call | solution.py:987
  50.4 2.0 %adam.1 = (f32[1024,128]{1,0:T(8,128)}, f32[256,32]{1,0:T(8,128)}, f32[64,512]{1,0:T(8,128)}, f32[512,512]{1,0:T(8,128)}, f32[3,512]{1,0:T(4,128)}) custom-call(f32[1024,128]{1,0:T(8,128)S(1)} %get-tuple-element.21.fine_step, f32[256,32]{1,0:T(8,128)S(1)} %get-tuple-element.22.coarse_step, f32[2,1024,128]{2,1,0:T(8,128)S(1)} %get-tuple-element.23.mid_full, ...), custom_call_target="tpu_custom_call" | custom-call | tf_op jit(solution)/shard_map/adam/pallas_call | solution.py:999

commit v4 on v3

--- a/solution.py
+++ b/solution.py
@@ -72,22 +72,29 @@
 
 class Links:
     def __init__(self, send, recv):
-        self.send, self.recv, self.used = send, recv, 0
-
-    def take(self, count):
-        first = self.used
-        self.used += count
-        return first
-
-    def copy(self, source, target, device, slot):
+        self.send, self.recv, self.sends, self.recvs = send, recv, 0, 0
+
+    def take(self):
+        self.recvs += 1
+        return self.recvs - 1
+
+    def take_send(self):
+        self.sends += 1
+        return self.sends - 1
+
+    def copy(self, source, target, device, slot, send):
         return pltpu.make_async_remote_copy(
             src_ref=source,
             dst_ref=target,
-            send_sem=self.send.at[slot],
+            send_sem=self.send.at[send],
             recv_sem=self.recv.at[slot],
             device_id=device,
             device_id_type=MESH,
         )
+
+    def wait(self, sent, landed, device, slot, send):
+        self.copy(sent, sent, device, slot, send).wait_send()
+        self.copy(landed, landed, device, slot, send).wait_recv()
 
 
 class Scatter:
@@ -98,106 +105,86 @@
             start, rows = self.spans[-1]
             part = rows // axis.size
             self.spans.append((start + axis.me * part, part))
-        self.slots = [links.take(axis.size - 1) for axis in axes]
-
-    def copies(self, stage):
-        axis, land = self.axes[stage], self.lands[stage]
-        start = self.spans[stage][0]
-        part = self.spans[stage + 1][1]
-        found = []
+        self.slots = [links.take() for axis in axes]
+        self.send = links.take_send()
+
+    def start(self, stage):
+        axis, start, part = self.axes[stage], self.spans[stage][0], self.spans[stage + 1][1]
         for step in range(1, axis.size):
             peer = axis.peer(step)
-            found.append(
-                self.links.copy(
-                    self.own.at[pl.ds(aligned(start + peer * part), part)],
-                    land.at[step - 1],
-                    axis.device(peer),
-                    self.slots[stage] + step - 1,
-                )
-            )
-        return found
-
-    def start(self, stage):
-        for copy in self.copies(stage):
-            copy.start()
+            self.links.copy(
+                self.own.at[pl.ds(aligned(start + peer * part), part)],
+                self.lands[stage].at[step - 1],
+                axis.device(peer),
+                self.slots[stage],
+                self.send,
+            ).start()
 
     def finish(self, stage):
+        axis, land = self.axes[stage], self.lands[stage]
         start, part = self.spans[stage + 1]
+        if axis.size > 1:
+            sent = self.own.at[pl.ds(0, (axis.size - 1) * part)]
+            device = axis.device(axis.peer(1))
+            self.links.wait(sent, land, device, self.slots[stage], self.send)
         span = pl.ds(aligned(start), part)
-        for step, copy in enumerate(self.copies(stage)):
-            copy.wait()
-            self.own[span] += self.lands[stage][step]
+        found = self.own[span]
+        for step in range(axis.size - 1):
+            found = found + land[step]
+        self.own[span] = found
 
 
 class Gather:
     def __init__(self, scatter, full):
         self.scatter, self.full = scatter, full
-        self.slots = [scatter.links.take(axis.size - 1) for axis in scatter.axes]
+        self.slots = [scatter.links.take() for axis in scatter.axes]
 
     def place(self):
         start, rows = self.scatter.spans[-1]
         span = pl.ds(aligned(start), rows)
         self.full[span] = self.scatter.own[span]
 
-    def copies(self, stage):
+    def start(self, stage):
         axis = self.scatter.axes[stage]
         start, rows = self.scatter.spans[stage + 1]
         block = self.full.at[pl.ds(aligned(start), rows)]
-        return [
+        for step in range(1, axis.size):
+            device = axis.device(axis.peer(step))
             self.scatter.links.copy(
-                block, block, axis.device(axis.peer(step)), self.slots[stage] + step - 1
-            )
-            for step in range(1, axis.size)
-        ]
-
-    def start(self, stage):
-        for copy in self.copies(stage):
-            copy.start()
+                block, block, device, self.slots[stage], self.scatter.send
+            ).start()
 
     def finish(self, stage):
-        for copy in self.copies(stage):
-            copy.wait()
-
-
-class Crowd:
-    def __init__(self, links, axis, source, target):
-        self.links, self.axis, self.slot = links, axis, links.take(1)
-        self.source, self.target = source, target
-
-    def start(self):
-        @pl.loop(1, self.axis.size)
-        def _(step):
-            peer = self.axis.peer(step)
-            self.links.copy(
-                self.source(peer), self.target(self.axis.me), self.axis.device(peer), self.slot
-            ).start()
-
-    def wait(self, sent, landed):
-        if self.axis.size > 1:
-            device = self.axis.device(self.axis.peer(1))
-            self.links.copy(sent, sent, device, self.slot).wait_send()
-            self.links.copy(landed, landed, device, self.slot).wait_recv()
+        axis, rows = self.scatter.axes[stage], self.scatter.spans[stage + 1][1]
+        if axis.size > 1:
+            span = self.full.at[pl.ds(0, (axis.size - 1) * rows)]
+            device = axis.device(axis.peer(1))
+            self.scatter.links.wait(span, span, device, self.slots[stage], self.scatter.send)
 
 
 class Total:
     def __init__(self, links, mine, lands, axes):
-        self.mine, self.lands, self.axes = mine, lands, axes
-        self.crowds = [
-            Crowd(links, axis, lambda peer: mine, lambda me, land=land: land.at[me])
-            for axis, land in zip(axes, lands)
-        ]
+        self.links, self.mine, self.lands, self.axes = links, mine, lands, axes
+        self.slots = [links.take() for axis in axes]
+        self.send = links.take_send()
         self.stage = 0
 
     def start(self):
-        self.lands[self.stage][self.axes[self.stage].me] = self.mine[...]
-        self.crowds[self.stage].start()
+        axis, land, slot = self.axes[self.stage], self.lands[self.stage], self.slots[self.stage]
+        land[axis.me] = self.mine[...]
+
+        @pl.loop(1, axis.size)
+        def _(step):
+            device = axis.device(axis.peer(step))
+            self.links.copy(self.mine, land.at[axis.me], device, slot, self.send).start()
 
     def finish(self):
-        land, count = self.lands[self.stage], self.axes[self.stage].size
-        span = land.at[pl.ds(0, max(count - 1, 1))]
-        self.crowds[self.stage].wait(span, span)
+        axis, land, slot = self.axes[self.stage], self.lands[self.stage], self.slots[self.stage]
+        if axis.size > 1:
+            span = land.at[pl.ds(0, axis.size - 1)]
+            self.links.wait(span, span, axis.device(axis.peer(1)), slot, self.send)
         total = land[0]
-        for place in range(1, count):
+        for place in range(1, axis.size):
             total = total + land[place]
         self.stage += 1
         if self.stage < len(self.axes):
@@ -321,13 +308,14 @@
     for place in (1, 2, 3, 4, 5, 0):
         loads_early[place].start()
     barrier = pltpu.get_barrier_semaphore()
-    expected = sum(axis.size - 1 for axis in axes)
-    for axis in axes:
+    z_near = ((z_at > 0, (row - 2, col)), (z_at < axis_z.size - 1, (row + 2, col)))
+    expected = sum(axis.size - 1 for axis in axes[:3])
+    for axis in axes[:3]:
         for step in range(1, axis.size):
             pl.semaphore_signal(
                 barrier, inc=1, device_id=axis.device(axis.peer(step)), device_id_type=MESH
             )
-    for there, device in near.values():
+    for there, device in list(near.values()) + list(z_near):
         expected = expected + there.astype(jnp.int32)
 
         @pl.when(there)
@@ -350,13 +338,23 @@
         return pltpu.roll(value, shift % LANES, 1)
 
     coarse_s[...] = jnp.zeros(coarse_s.shape, F32)
-    up_buf[...] = jnp.zeros(up_buf.shape, F32)
     loads_early[1].wait()
     loads_early[2].wait()
     for r in range(CR):
         coarse_s[r, :, :CC] = coarse[pl.ds(r, CH, stride=CR), :]
-    up_buf[0] = fine_row(0)
-    up_buf[1] = coarse_s[0]
+    up_buf[:CH] = fine_row(0)
+    group = CH * CC // LANES
+    side = [slice(k * group, (k + 1) * group) for k in range(LANES // CC)]
+
+    def pack(value):
+        return sum(roll(value[side[k]], k * CC) for k in range(LANES // CC))
+
+    def unpack(value, target):
+        kept = lax.broadcasted_iota(jnp.int32, (group, LANES), 1) < CC
+        for k in range(LANES // CC):
+            target[side[k]] = jnp.where(kept, roll(value, -k * CC), 0.0)
+
+    up_buf[CH:] = pack(coarse_s[0])
     packed = jnp.zeros((CH, LANES), F32)
     for r in range(SR):
         packed = jnp.where(lane == r, roll(fine_row(r), r), packed)
@@ -366,10 +364,14 @@
 
     pl.semaphore_wait(barrier, expected)
 
+    halo_sends = [links.take_send() for _ in range(6)]
+    halos_used = [0]
+
     def halo(source, target, towards, back):
-        slot = links.take(1)
-        copy = links.copy(source, target, near[towards][1], slot)
-        arriving = links.copy(source, target, near[back][1], slot)
+        slot, send = links.take(), halo_sends[halos_used[0] % 6]
+        halos_used[0] += 1
+        copy = links.copy(source, target, near[towards][1], slot, send)
+        arriving = links.copy(source, target, near[back][1], slot, send)
 
         @pl.when(near[towards][0])
         def _():
@@ -420,12 +422,13 @@
         wait()
 
     for r in range(SR + 1):
-        value = fine_row(r) if r < SR else below_buf[0]
+        value = fine_row(r) if r < SR else below_buf[:CH]
         edge = roll(right_cp[...], LANES - 1 - r) if r < SR else roll(diag_cp[...], LANES - 1)
         shifted = jnp.where(lane == LANES - 1, edge, roll(value, LANES - 1))
         across[r] = (1.0 - off_x) * value + off_x * shifted
+    unpack(below_buf[CH:], coarse_s.at[CR])
     for r in range(CR + 1):
-        value = coarse_s[r] if r < CR else below_buf[1]
+        value = coarse_s[r]
         edge = roll(right_cp[...], CC - SR - r) if r < CR else roll(diag_cp[...], CC - SR)
         coarse_s[r] = jnp.where(lane == CC, edge, value)
     across_c[...] = dot(
@@ -435,17 +438,33 @@
     def chunk_span(c):
         return slice(c * CHUNK, (c + 1) * CHUNK)
 
-    def spread_word(place, axis):
-        for step in range(1, axis.size):
-            pl.semaphore_signal(
-                know_sem.at[place],
-                inc=1,
-                device_id=axis.device(axis.peer(step)),
-                device_id_type=MESH,
-            )
-
-    def hear_word(place, axis):
-        pl.semaphore_wait(know_sem.at[place], axis.size - 1)
+    def tell(place, targets):
+        for there, device in targets:
+
+            @pl.when(there)
+            def _():
+                pl.semaphore_signal(
+                    know_sem.at[place], inc=1, device_id=device, device_id_type=MESH
+                )
+
+    def hear(place, targets):
+        pl.semaphore_wait(know_sem.at[place], sum(there.astype(jnp.int32) for there, _ in targets))
+
+    def peers_of(axis):
+        always = row >= 0
+        return [(always, axis.device(axis.peer(step))) for step in range(1, axis.size)]
+
+    words = [z_near] * max(axis_z.size - 2, 0) + [peers_of(axis_x), peers_of(axis_y)]
+    words = [targets for targets in words if targets]
+    heard = [0]
+
+    def pass_word(count):
+        for _ in range(count):
+            if heard[0] < len(words):
+                hear(heard[0], words[heard[0]])
+                heard[0] += 1
+                if heard[0] < len(words):
+                    tell(heard[0], words[heard[0]])
 
     def forward(c):
         for k in range(GROUP):
@@ -485,17 +504,15 @@
             halo(col_send.at[batch, pl.ds(1, 2)], col_recv.at[batch, pl.ds(1, 2)], "right", "left"),
         ]
 
-    spread_word(0, axis_x)
+    tell(0, words[0])
     for place in range(CHUNKS - 1):
         forward(order[place])
-        if place == 0:
-            hear_word(0, axis_x)
-            spread_word(1, axis_y)
-    hear_word(1, axis_y)
+        pass_word(-(-len(words) // CHUNKS))
     loads_early[0].wait()
     edge_send[0, 0] = pred[1]
     edge_send[1, 0] = pred[SR]
     edge_send[1, 1] = target_row(1, SR - 1)
+    halos_used[0] = 0
     early_waits = [
         halo(edge_send.at[0, 0], edge_recv.at[0, 0], "up", "down"),
         halo(edge_send.at[1], edge_recv.at[1], "down", "up"),
@@ -508,6 +525,7 @@
             edge_recv[place] = jnp.zeros(edge_recv.shape[1:], F32)
 
     forward(order[-1])
+    pass_word(len(words))
     last_waits = send_columns(1, order[-1:])
     for place, back in ((0, "right"), (1, "left"), (2, "left")):
 
@@ -516,6 +534,9 @@
             for batch in range(2):
                 col_recv[batch, place] = jnp.zeros(col_recv.shape[2:], F32)
 
+    ready = order[:2]
+    for c in ready:
+        half_1[:, chunk_span(c)] = slope_of_half(half_1[:, chunk_span(c)])
     for wait in early_waits:
         wait()
     pred[SR + 1] = edge_recv[0, 0]
@@ -552,7 +573,7 @@
 
     def upper(c):
         span = chunk_span(c)
-        slope = slope_of_half(half_1[:, span])
+        slope = half_1[:, span] if c in ready else slope_of_half(half_1[:, span])
         delta_1[:, span] = (dot(b_out_t[...], cot_s[:, span]) * slope).astype(BF16)
 
     for c in order[:-1]:
@@ -587,7 +608,11 @@
     part_span = lambda k: pl.ds(k * part_rows, part_rows)
     pairs = [
         links.copy(
-            mid_away.at[part_span(k)], mid_pair.at[part_span(k)], partner, links.take(1)
+            mid_away.at[part_span(k)],
+            mid_pair.at[part_span(k)],
+            partner,
+            links.take(),
+            mids[k].send,
         )
         for k in range(parts)
     ]
@@ -647,7 +672,7 @@
             target[in_rows:, :] = jnp.zeros((target.shape[0] - in_rows, LANES), F32)
 
     in_half(1 - core, in_away)
-    pair_in = links.copy(in_away, in_pair, partner, links.take(1))
+    pair_in = links.copy(in_away, in_pair, partner, links.take(), mids[parts].send)
     pair_in.start()
     in_half(core, in_own)
 
@@ -670,7 +695,7 @@
         if r < SR:
             fine_g[r] = out
         else:
-            down_buf[0] = out
+            down_buf[:CH] = out
     for j in range(CR + 1):
         value = zero
         for k in range(RATIO):
@@ -691,8 +716,9 @@
         if j < CR:
             coarse_g[j] = value
         else:
-            down_buf[1] = value
+            down_buf[CH:] = pack(value)
     q_buf[...] = packed
+    halos_used[0] = 0
     waits = [
         halo(down_buf, above_buf, "down", "up"),
         halo(q_buf, left_q, "right", "left"),
@@ -728,8 +754,9 @@
     settle((0, 1))
     for wait in waits:
         wait()
-    fine_g[0] += above_buf[0] + jnp.where(lane == 0, roll(diag_q[...], -(SR + CR)), 0.0)
-    coarse_g[0] += above_buf[1] + jnp.where(lane == 0, roll(diag_q[...], -(SR + CR + 1)), 0.0)
+    fine_g[0] += above_buf[:CH] + jnp.where(lane == 0, roll(diag_q[...], -(SR + CR)), 0.0)
+    unpack(above_buf[CH:], coarse_s.at[0])
+    coarse_g[0] += coarse_s[0] + jnp.where(lane == 0, roll(diag_q[...], -(SR + CR + 1)), 0.0)
     squares = jnp.zeros((CH, LANES), F32)
     for r in range(SR):
         value = fine_g[r] + jnp.where(lane == 0, roll(left_q[...], -r), 0.0)
@@ -772,7 +799,7 @@
         )
     def across_pair(k):
         block = mid_full.at[core, part_span(k)]
-        copy = links.copy(block, block, partner, links.take(1))
+        copy = links.copy(block, block, partner, links.take(), mids[k].send)
         copy.start()
         return copy
 
@@ -782,12 +809,13 @@
         lasts.append(across_pair(k))
         if k == 1:
             gathers[parts].finish(0)
-            last_in = links.copy(in_full.at[core], in_full.at[core], partner, links.take(1))
+            block = in_full.at[core]
+            last_in = links.copy(block, block, partner, links.take(), mids[parts].send)
             last_in.start()
             lasts.append(last_in)
     for copy in lasts:
         copy.wait()
-    assert links.used <= dims["COPIES"]
+    assert (links.sends, links.recvs) == (dims["SENDS"], dims["RECVS"])
 
 
 def adam_kernel(
@@ -886,14 +914,13 @@
     S = SR * SC
     rows_n, cols_n = lax.axis_size("row"), lax.axis_size("col")
     sizes_x, sizes_y, sizes_z = 2, cols_n // 2, rows_n // 2
-    peers = (sizes_x - 1) + (sizes_y - 1) + (sizes_z - 1)
     parts = 4
-    copies = 2 * parts * (peers + 1) + 2 * (sizes_x * sizes_y + sizes_z) + 24
+    sends, recvs = 6 + parts + 1 + 2, 12 + 6 + 2 * (parts + 1) + 2 * (3 * parts + 2)
     chips = sizes_x * sizes_y * sizes_z
     in_rows = CH * HID // LANES
     in_rows = -(-in_rows // (chips * SUBLANES)) * chips * SUBLANES
     mid_rows = HID * HID // 2 // LANES
-    dims = dict(CH=CH, SR=SR, SC=SC, CR=CR, CC=CC, HID=HID, OUT=OUT, COPIES=copies, GROUP=8)
+    dims = dict(CH=CH, SR=SR, SC=SC, CR=CR, CC=CC, HID=HID, OUT=OUT, SENDS=sends, RECVS=recvs, GROUP=8)
 
     flat = lambda grid: grid.reshape(-1, grid.shape[-1])
     early = (
@@ -917,12 +944,13 @@
 
     orders = ((sizes_x, sizes_y, sizes_z), (sizes_y, sizes_x, sizes_z))
     kept = (in_first.T, in_second.T, mid_first[0], mid_second[0], out_first, out_second)
+    edge = CH + CH * CC // LANES
     scratch = [pltpu.SMEM(offsets.shape, jnp.int32)]
     scratch += [pltpu.VMEM(a.shape, F32) for a in early + late]
     scratch += [
-        vmem(2, CH, LANES),
+        vmem(edge, LANES),
         vmem(CH, LANES),
-        vmem(2, CH, LANES),
+        vmem(edge, LANES),
         vmem(CH, LANES),
         vmem(CH, LANES),
         vmem(CR + 1, CH, LANES),
@@ -947,9 +975,9 @@
         vmem(2, 3, SUBLANES, LANES),
         low(SUBLANES, S),
         vmem(SR, 2 * CH, LANES),
-        vmem(2, CH, LANES),
+        vmem(edge, LANES),
         vmem(CH, LANES),
-        vmem(2, CH, LANES),
+        vmem(edge, LANES),
         vmem(CH, LANES),
         vmem(CH, LANES),
         vmem(SR, CH, LANES),
@@ -971,9 +999,9 @@
     scratch += landing(in_rows, (sizes_x * sizes_y, sizes_z))
     scratch += [
         pltpu.SemaphoreType.DMA((len(early) + len(late) + len(kept) + 1,)),
-        pltpu.SemaphoreType.DMA((copies,)),
-        pltpu.SemaphoreType.DMA((copies,)),
-        pltpu.SemaphoreType.REGULAR((2,)),
+        pltpu.SemaphoreType.DMA((sends,)),
+        pltpu.SemaphoreType.DMA((recvs,)),
+        pltpu.SemaphoreType.REGULAR((max(sizes_z - 2, 0) + 2,)),
     ]
     outs = (
         (CH * SR, SC),
@@ -1002,7 +1030,7 @@
         in_specs=[whole] * len(found),
         out_specs=[far] * len(steps),
         scratch_shapes=[pltpu.VMEM(shape, F32) for shape in steps[2:]]
-        + [pltpu.SemaphoreType.DMA((4 + 2 * HID // LANES,))],
+        + [pltpu.SemaphoreType.DMA((6,))],
         compiler_params=pltpu.CompilerParams(vmem_limit_bytes=8 * 1024 * 1024),
         name="adam",
     )(*found)

time: 52.7 us -> 49.6 us (0.941)
  Pallas kernels: 51.7 us -> 48.6 us
    pallas_call x1, Pallas kernels: 49.7 us -> 46.7 us  [shards(): pl.pallas_call(functools.partial(step_kernel, dims), out_shape=[jax.Shape...]
where the time goes in v4:
time: 49.6 us; the launch traced here: 49.4 us
  Pallas kernels  48.6 us (98%)
  between operations  0.83 us (2%)
    pallas_call x1, Pallas kernels, shards(): pl.pallas_call(functools.partial(step_kernel, dims), out_shape=[jax.Shape...  46.7 us
    pallas_call x1, Pallas kernels, shards(): pl.pallas_call(adam_kernel, out_shape=[jax.ShapeDtypeStruct(shape, F32) f...  1.95 us

profile of v4, /device:TPU:0, one launch (start us, length us, event | category | flops | bytes accessed | tf_op | source)
XLA Modules:
  0.0 49.4 jit_solution(11850242061258661027)
XLA Ops:
  0.6 46.7 %field.1 = (f32[1024,128]{1,0:T(8,128)S(1)}, f32[256,32]{1,0:T(8,128)S(1)}, f32[2,1024,128]{2,1,0:T(8,128)S(1)}, f32[2,128,128]{2,1,0:T(8,128)S(1)}, f32[3,512]{...) custom-call(s32[1,1,2]{2,1,0:T(1,128)} %refs_0_.1, ...), custom_call_target="tpu_custom_call" | custom-call | tf_op jit(solution)/shard_map/field/pallas_call | solution.py:1015
  47.3 2.0 %adam.1 = (f32[1024,128]{1,0:T(8,128)}, f32[256,32]{1,0:T(8,128)}, f32[64,512]{1,0:T(8,128)}, f32[512,512]{1,0:T(8,128)}, f32[3,512]{1,0:T(4,128)}) custom-call(f32[1024,128]{1,0:T(8,128)S(1)} %get-tuple-element.21.fine_step, f32[256,32]{1,0:T(8,128)S(1)} %get-tuple-element.22.coarse_step, f32[2,1024,128]{2,1,0:T(8,128)S(1)} %get-tuple-element.23.mid_full, ...), custom_call_target="tpu_custom_call" | custom-call | tf_op jit(solution)/shard_map/adam/pallas_call | solution.py:1027

commit v5 on v4

--- a/solution.py
+++ b/solution.py
@@ -36,7 +36,7 @@
     )
     root = gradient * (clip_scale * ((1.0 - BETA_TWO) * rise_two) ** 0.5)
     new_two = (BETA_TWO * rise_two) * moment_two + root * root
-    return new_one / (jnp.sqrt(new_two) + ADAM_EPSILON)
+    return new_one / (new_two * lax.rsqrt(new_two) + ADAM_EPSILON)
 
 
 def dot(former, latter, dims=((1,), (0,)), precision=None):
@@ -137,7 +137,12 @@
 class Gather:
     def __init__(self, scatter, full):
         self.scatter, self.full = scatter, full
+        self.axes, self.spans = scatter.axes, scatter.spans
         self.slots = [scatter.links.take() for axis in scatter.axes]
+
+    def flatten(self, axis):
+        self.axes, self.spans = [axis], [None, self.scatter.spans[-1]]
+        return self
 
     def place(self):
         start, rows = self.scatter.spans[-1]
@@ -145,8 +150,8 @@
         self.full[span] = self.scatter.own[span]
 
     def start(self, stage):
-        axis = self.scatter.axes[stage]
-        start, rows = self.scatter.spans[stage + 1]
+        axis = self.axes[stage]
+        start, rows = self.spans[stage + 1]
         block = self.full.at[pl.ds(aligned(start), rows)]
         for step in range(1, axis.size):
             device = axis.device(axis.peer(step))
@@ -155,7 +160,7 @@
             ).start()
 
     def finish(self, stage):
-        axis, rows = self.scatter.axes[stage], self.scatter.spans[stage + 1][1]
+        axis, rows = self.axes[stage], self.spans[stage + 1][1]
         if axis.size > 1:
             span = self.full.at[pl.ds(0, (axis.size - 1) * rows)]
             device = axis.device(axis.peer(1))
@@ -252,7 +257,7 @@
     ) = take(43)
     out_lands = take(4)
     total_lands = take(2)
-    lands = take(14)
+    lands = take(2 * dims["PARTS"] + 2)
     load_sem, send_sem, recv_sem, know_sem = take(4)
 
     rows_n, cols_n = lax.axis_size("row"), lax.axis_size("col")
@@ -587,15 +592,15 @@
 
     half = HID // 2
     mid_rows = HID * half // LANES
-    parts = 4
+    parts = dims["PARTS"]
     part_rows = mid_rows // parts
-    orders = ((axis_x, axis_y, axis_z), (axis_y, axis_x, axis_z))
+    ahead, behind = tuple(range(-(-parts // 2))), tuple(range(-(-parts // 2), parts))
     mids = [
-        Scatter(links, mid_own, k * part_rows, part_rows, orders[k % 2], lands[k * 3 : k * 3 + 3])
+        Scatter(links, mid_own, k * part_rows, part_rows, (axis_plane, axis_z), lands[k * 2 : k * 2 + 2])
         for k in range(parts)
     ]
     mids.append(
-        Scatter(links, in_own, 0, in_own.shape[0], (axis_plane, axis_z), lands[3 * parts :])
+        Scatter(links, in_own, 0, in_own.shape[0], (axis_plane, axis_z), lands[2 * parts :])
     )
 
     def mid_half(which, target):
@@ -648,12 +653,10 @@
     half_chunks = CHUNKS // 2
     for c in range(half_chunks):
         lower(c)
-    outs.finish()
-    advance((0, 1), 0)
     for c in range(half_chunks, CHUNKS - 1):
         lower(c)
     outs.finish()
-    advance((2, 3), 0)
+    advance(ahead, 0)
     lower(CHUNKS - 1)
 
     blocks = HID // LANES
@@ -675,8 +678,6 @@
     pair_in = links.copy(in_away, in_pair, partner, links.take(), mids[parts].send)
     pair_in.start()
     in_half(core, in_own)
-
-    advance((0, 1), 1)
 
     last = SR
     bottom = None
@@ -696,6 +697,11 @@
             fine_g[r] = out
         else:
             down_buf[:CH] = out
+    outs.finish()
+    advance(behind, 0)
+    pair_in.wait()
+    in_own[...] += in_pair[...]
+    mids[parts].start(0)
     for j in range(CR + 1):
         value = zero
         for k in range(RATIO):
@@ -730,20 +736,15 @@
         def _():
             target[...] = jnp.zeros(target.shape, F32)
 
-    advance((2, 3), 1)
-    outs.finish()
-    pair_in.wait()
-    in_own[...] += in_pair[...]
-    mids[parts].start(0)
     gathers = [Gather(scatter, mid_full.at[core]) for scatter in mids[:parts]]
-    gathers.append(Gather(mids[parts], in_full.at[core]))
+    gathers.append(Gather(mids[parts], in_full.at[core]).flatten(axis_chips))
 
     def settle(which):
         for k in which:
             last_stage = len(mids[k].axes) - 1
             mids[k].finish(last_stage)
             gathers[k].place()
-            gathers[k].start(last_stage)
+            gathers[k].start(len(gathers[k].axes) - 1)
 
     def regain(which, stage):
         for k in which:
@@ -751,7 +752,7 @@
             if stage > 0:
                 gathers[k].start(stage - 1)
 
-    settle((0, 1))
+    settle(ahead)
     for wait in waits:
         wait()
     fine_g[0] += above_buf[:CH] + jnp.where(lane == 0, roll(diag_q[...], -(SR + CR)), 0.0)
@@ -772,16 +773,14 @@
     total_mine[...] = jnp.sum(total, axis=0, keepdims=True)
     totals = Total(links, total_mine, total_lands, (axis_core, axis_chips))
     totals.start()
+    outs.finish()
+    settle(behind)
     advance((parts,), 0)
-    settle((2, 3))
     totals.finish()
-    regain((0, 1), 2)
+    regain(ahead, 1)
+    regain(behind, 1)
     settle((parts,))
     out_full[...] = outs.finish()
-    regain((2, 3), 2)
-    regain((0, 1), 1)
-    regain((2, 3), 1)
-    regain((parts,), 1)
     grid_total = totals.finish()
 
     for load in loads_late:
@@ -804,15 +803,17 @@
         return copy
 
     lasts = []
-    for k in range(parts):
+    for k in ahead:
         gathers[k].finish(0)
         lasts.append(across_pair(k))
-        if k == 1:
-            gathers[parts].finish(0)
-            block = in_full.at[core]
-            last_in = links.copy(block, block, partner, links.take(), mids[parts].send)
-            last_in.start()
-            lasts.append(last_in)
+    for k in behind:
+        gathers[k].finish(0)
+        lasts.append(across_pair(k))
+    gathers[parts].finish(0)
+    block = in_full.at[core]
+    last_in = links.copy(block, block, partner, links.take(), mids[parts].send)
+    last_in.start()
+    lasts.append(last_in)
     for copy in lasts:
         copy.wait()
     assert (links.sends, links.recvs) == (dims["SENDS"], dims["RECVS"])
@@ -914,13 +915,13 @@
     S = SR * SC
     rows_n, cols_n = lax.axis_size("row"), lax.axis_size("col")
     sizes_x, sizes_y, sizes_z = 2, cols_n // 2, rows_n // 2
-    parts = 4
-    sends, recvs = 6 + parts + 1 + 2, 12 + 6 + 2 * (parts + 1) + 2 * (3 * parts + 2)
+    parts = max(1, min(4, HID * HID // 2 // LANES // (sizes_x * sizes_y * sizes_z * SUBLANES)))
+    sends, recvs = 6 + parts + 1 + 2, 12 + 6 + 2 * (parts + 1) + 2 * (2 * parts + 2)
     chips = sizes_x * sizes_y * sizes_z
     in_rows = CH * HID // LANES
     in_rows = -(-in_rows // (chips * SUBLANES)) * chips * SUBLANES
     mid_rows = HID * HID // 2 // LANES
-    dims = dict(CH=CH, SR=SR, SC=SC, CR=CR, CC=CC, HID=HID, OUT=OUT, SENDS=sends, RECVS=recvs, GROUP=8)
+    dims = dict(CH=CH, SR=SR, SC=SC, CR=CR, CC=CC, HID=HID, OUT=OUT, PARTS=parts, SENDS=sends, RECVS=recvs, GROUP=8)
 
     flat = lambda grid: grid.reshape(-1, grid.shape[-1])
     early = (
@@ -942,7 +943,6 @@
             found.append(vmem(max(size - 1, 1), rows, LANES))
         return found
 
-    orders = ((sizes_x, sizes_y, sizes_z), (sizes_y, sizes_x, sizes_z))
     kept = (in_first.T, in_second.T, mid_first[0], mid_second[0], out_first, out_second)
     edge = CH + CH * CC // LANES
     scratch = [pltpu.SMEM(offsets.shape, jnp.int32)]
@@ -995,7 +995,7 @@
     scratch += [vmem(size, OUT, HID) for size in (2, sizes_x, sizes_y, sizes_z)]
     scratch += [vmem(size, 1, LANES) for size in (2, chips)]
     for part in range(parts):
-        scratch += landing(mid_rows // parts, orders[part % 2])
+        scratch += landing(mid_rows // parts, (sizes_x * sizes_y, sizes_z))
     scratch += landing(in_rows, (sizes_x * sizes_y, sizes_z))
     scratch += [
         pltpu.SemaphoreType.DMA((len(early) + len(late) + len(kept) + 1,)),

time: 49.6 us -> 46.4 us (0.935)
  Pallas kernels: 48.6 us -> 45.5 us
    pallas_call x1, Pallas kernels: 46.7 us -> 43.6 us  [shards(): pl.pallas_call(functools.partial(step_kernel, dims), out_shape=[jax.Shape...]
where the time goes in v5:
time: 46.4 us; the launch traced here: 46.3 us
  Pallas kernels  45.5 us (98%)
  between operations  0.83 us (2%)
    pallas_call x1, Pallas kernels, shards(): pl.pallas_call(functools.partial(step_kernel, dims), out_shape=[jax.Shape...  43.6 us
    pallas_call x1, Pallas kernels, shards(): pl.pallas_call(adam_kernel, out_shape=[jax.ShapeDtypeStruct(shape, F32) f...  1.82 us

profile of v5, /device:TPU:0, one launch (start us, length us, event | category | flops | bytes accessed | tf_op | source)
XLA Modules:
  0.0 46.3 jit_solution(12143699576895256257)
XLA Ops:
  0.6 43.6 %field.1 = (f32[1024,128]{1,0:T(8,128)S(1)}, f32[256,32]{1,0:T(8,128)S(1)}, f32[2,1024,128]{2,1,0:T(8,128)S(1)}, f32[2,128,128]{2,1,0:T(8,128)S(1)}, f32[3,512]{...) custom-call(s32[1,1,2]{2,1,0:T(1,128)} %refs_0_.1, ...), custom_call_target="tpu_custom_call" | custom-call | tf_op jit(solution)/shard_map/field/pallas_call | solution.py:1015
  44.3 1.8 %adam.1 = (f32[1024,128]{1,0:T(8,128)}, f32[256,32]{1,0:T(8,128)}, f32[64,512]{1,0:T(8,128)}, f32[512,512]{1,0:T(8,128)}, f32[3,512]{1,0:T(4,128)}) custom-call(f32[1024,128]{1,0:T(8,128)S(1)} %get-tuple-element.21.fine_step, f32[256,32]{1,0:T(8,128)S(1)} %get-tuple-element.22.coarse_step, f32[2,1024,128]{2,1,0:T(8,128)S(1)} %get-tuple-element.23.mid_full, ...), custom_call_target="tpu_custom_call" | custom-call | tf_op jit(solution)/shard_map/adam/pallas_call | solution.py:1027

commit v6 on v5

--- a/solution.py
+++ b/solution.py
@@ -684,6 +684,9 @@
     packed = jnp.zeros((CH, LANES), F32)
     zero = jnp.zeros((CH, LANES), F32)
     for r in range(SR + 1):
+        if r == SR // 2:
+            outs.finish()
+            advance(behind, 0)
         value = zero
         if r < SR:
             value = (1.0 - off_y) * fgrad[r, :CH]
@@ -697,8 +700,6 @@
             fine_g[r] = out
         else:
             down_buf[:CH] = out
-    outs.finish()
-    advance(behind, 0)
     pair_in.wait()
     in_own[...] += in_pair[...]
     mids[parts].start(0)
@@ -753,6 +754,7 @@
                 gathers[k].start(stage - 1)
 
     settle(ahead)
+    settle(behind)
     for wait in waits:
         wait()
     fine_g[0] += above_buf[:CH] + jnp.where(lane == 0, roll(diag_q[...], -(SR + CR)), 0.0)
@@ -774,7 +776,6 @@
     totals = Total(links, total_mine, total_lands, (axis_core, axis_chips))
     totals.start()
     outs.finish()
-    settle(behind)
     advance((parts,), 0)
     totals.finish()
     regain(ahead, 1)

time: 46.4 us -> 46.5 us (level)
  no operation moved by 1% of the time
where the time goes in v6:
time: 46.5 us; the launch traced here: 46.4 us
  Pallas kernels  45.6 us (98%)
  between operations  0.83 us (2%)
    pallas_call x1, Pallas kernels, shards(): pl.pallas_call(functools.partial(step_kernel, dims), out_shape=[jax.Shape...  43.8 us
    pallas_call x1, Pallas kernels, shards(): pl.pallas_call(adam_kernel, out_shape=[jax.ShapeDtypeStruct(shape, F32) f...  1.82 us

profile of v6, /device:TPU:0, one launch (start us, length us, event | category | flops | bytes accessed | tf_op | source)
XLA Modules:
  0.0 46.4 jit_solution(13345921232707531889)
XLA Ops:
  0.6 43.8 %field.1 = (f32[1024,128]{1,0:T(8,128)S(1)}, f32[256,32]{1,0:T(8,128)S(1)}, f32[2,1024,128]{2,1,0:T(8,128)S(1)}, f32[2,128,128]{2,1,0:T(8,128)S(1)}, f32[3,512]{...) custom-call(s32[1,1,2]{2,1,0:T(1,128)} %refs_0_.1, ...), custom_call_target="tpu_custom_call" | custom-call | tf_op jit(solution)/shard_map/field/pallas_call | solution.py:1016
  44.4 1.8 %adam.1 = (f32[1024,128]{1,0:T(8,128)}, f32[256,32]{1,0:T(8,128)}, f32[64,512]{1,0:T(8,128)}, f32[512,512]{1,0:T(8,128)}, f32[3,512]{1,0:T(4,128)}) custom-call(f32[1024,128]{1,0:T(8,128)S(1)} %get-tuple-element.21.fine_step, f32[256,32]{1,0:T(8,128)S(1)} %get-tuple-element.22.coarse_step, f32[2,1024,128]{2,1,0:T(8,128)S(1)} %get-tuple-element.23.mid_full, ...), custom_call_target="tpu_custom_call" | custom-call | tf_op jit(solution)/shard_map/adam/pallas_call | solution.py:1028
